TPU v7x, 32 devices: a whole 2x2x4 slice. The times are simulated.
32 devices in a mesh: dp: 4 (over x, core), center: 8 (over z, y).
Axes of the slice: x: 2, y: 2, z: 4, core: 2. Of those that a mesh axis runs over, the one named last changes fastest.
Arguments:
- features: bfloat16 [4096, 1024], P('dp'), may hold values from -6 to 6
- centers: bfloat16 [4096, 1024], P('center'), may hold values from -6 to 6
- targets: bfloat16 [4096, 256], P('dp'), may hold values from -6 to 6
Outputs:
- coef: float32 [4096, 256], P('center')
- residual: float32 [4096, 256], P('center')
All inputs are finite; a program needn't handle non-finite values.
Results may differ from a plain program's by a relative error of at most 0.024.
Values may be sent and summed in bfloat16 or wider, within the bound.
No kernel may reach another device: no remote copies, remote signals or barrier semaphores. Data moves between devices by JAX's collectives and lax.ppermute only.
A program may use at most 64 MiB of HBM per device.

v0:
```python
import functools
import math

import jax
import jax.numpy as jnp
from jax import lax
from jax.experimental import pallas as pl
from jax.experimental.pallas import tpu as pltpu
from jax.sharding import PartitionSpec as P


F32 = jnp.float32
BF16 = jnp.bfloat16
NT = (((1,), (1,)), ((), ()))
NN = (((1,), (0,)), ((), ()))
QUAD = 4
CORES = 2
TILE = 256
CHUNKS = 2
LANES = 128
WORDS = 3


def vmem_call(body, outs, scratch=(), flops=0, nbytes=0, limit=32 << 20, **kw):
    many = isinstance(outs, (list, tuple))
    return pl.pallas_call(
        body,
        out_shape=outs,
        scratch_shapes=list(scratch),
        out_specs=jax.tree.map(lambda _: pl.BlockSpec(memory_space=pltpu.VMEM), tuple(outs) if many else outs),
        compiler_params=pltpu.CompilerParams(vmem_limit_bytes=limit),
        cost_estimate=pl.CostEstimate(flops=flops, bytes_accessed=nbytes, transcendentals=0),
        **kw,
    )


def kernel_block(rows, centers):
    scores = lax.dot_general(rows, centers, NT, preferred_element_type=F32)
    lifted = 1.0 + 0.5 / math.sqrt(rows.shape[1]) * scores
    return (lifted * lifted * lifted).astype(BF16)


def times_kernel(low, refs, emit):
    for at in range(0, refs[0].shape[0], TILE):
        total, first = None, 0
        for ref in refs:
            width = ref.shape[1]
            term = lax.dot_general(
                ref[at : at + TILE, :], low[:, first : first + width], NT, preferred_element_type=F32
            )
            total = term if total is None else total + term
            first += width
        emit(slice(at, at + TILE), total.T)


def times_transposed(low, refs, store):
    first = 0
    for ref in refs:
        value = lax.dot_general(low, ref[...], NN, preferred_element_type=F32)
        store(slice(first, first + ref.shape[1]), value)
        first += ref.shape[1]


def side_kernel(first, second, one, two, out):
    out[...] = lax.dot_general(first[...], one[...], NN, preferred_element_type=F32)
    out[...] += lax.dot_general(second[...], two[...], NN, preferred_element_type=F32)


def right_kernel(scale, own, got, *out):
    w = out[0].shape[0]
    for hop in range(QUAD):
        rows = slice(hop * w, (hop + 1) * w)
        out[hop][...] = (own[rows, :] + got[rows, :]) * scale


def segments():
    found = []
    for chunk in range(CHUNKS):
        for far in range(CORES):
            found += [(1, far, chunk), (2, far, chunk)]
    for far in range(CORES):
        found += [(3, far, chunk) for chunk in range(CHUNKS)]
    return found


def early_kernel(count, n_early, *refs):
    sides, k_refs = refs[:QUAD], refs[QUAD : QUAD + count]
    right_side, low_last, partial = refs[QUAD + count :]
    core = lax.axis_index("dp") % CORES
    width = sides[0].shape[1]
    half = width // CORES
    cut = half // CHUNKS
    right_side[:, :width] = sides[0][...]
    for index, (hop, far, chunk) in enumerate(segments()):
        at = pl.multiple_of(jnp.bitwise_xor(core, far) * half + chunk * cut, cut)
        to = width + index * cut
        right_side[:, to : to + cut] = sides[hop][:, pl.ds(at, cut)]
    low_last[...] = right_side[:, n_early:].astype(BF16)

    def emit(cols, value):
        partial[:, cols] = value

    times_kernel(right_side[:, :n_early].astype(BF16), k_refs, emit)


def late_kernel(low, early, *refs):
    k_refs, (partial, partial_low) = refs[:-2], refs[-2:]

    def emit(cols, value):
        value = value + early[:, cols]
        partial[:, cols] = value
        partial_low[:, cols] = value.astype(BF16)

    times_kernel(low, k_refs, emit)


def second_kernel(direction, *refs):
    k_refs, (partial, partial_low) = refs[:-2], refs[-2:]

    def emit(cols, value):
        partial[:, cols] = value
        partial_low[:, cols] = value.astype(BF16)

    times_kernel(direction[...].astype(BF16), k_refs, emit)


def rounded(partial, got):
    total = partial[...] + got[...].astype(F32)
    low = total.astype(BF16)
    return low, jnp.sum(total * low.astype(F32), axis=1, keepdims=True)


def back_kernel(partial, got, *refs):
    k_refs, (image, squares) = refs[:-2], refs[-2:]
    low, sums = rounded(partial, got)
    squares[...] = jnp.broadcast_to(sums, squares.shape)

    def store(cols, value):
        image[:, cols] = value

    times_transposed(low, k_refs, store)


def back_rest_kernel(partial, got, before, *refs):
    k_refs, image = refs[:-1], refs[-1]
    low, _ = rounded(partial, got)

    def store(cols, value):
        image[:, cols] = before[:, cols] + value

    times_transposed(low, k_refs, store)


def back_last_kernel(partial, got, before, squares, *refs):
    k_refs, (image, image_low) = refs[:-2], refs[-2:]
    low, left = rounded(partial, got)
    left = left + squares[:, :1]
    tail = image_low.shape[1] - LANES
    lane = lax.broadcasted_iota(jnp.int32, (left.shape[0], LANES), 1)
    words = jnp.zeros(lane.shape, F32)
    for index in range(WORDS):
        word = left.astype(BF16).astype(F32)
        words = jnp.where(lane == index, word, words)
        left = left - word
    image_low[:, tail:] = words.astype(BF16)

    def store(cols, value):
        value = before[:, cols] + value
        image[:, cols] = value
        image_low[:, cols] = value.astype(BF16)

    times_transposed(low, k_refs, store)


def sums_kernel(rows, own, got, right_side, image, sums):
    direction = right_side[...]
    value = (own[...] + got[...]) * (1.0 / rows) + 0.5 * direction
    image[...] = value
    lane = lax.broadcasted_iota(jnp.int32, sums.shape, 1)
    found = jnp.zeros(sums.shape, F32)
    for index, product in enumerate((direction * direction, direction * value, value * value)):
        found = jnp.where(lane == index, jnp.sum(product, axis=1, keepdims=True), found)
    sums[...] = found


def scalars(own_sums, got_sums):
    total = own_sums[...] + got_sums[...]
    norm, curvature, image_sq = [total[:, k : k + 1] for k in range(3)]
    step = norm / (curvature + 1e-06)
    norm_next = norm - 2.0 * step * curvature + step * step * image_sq
    ratio = norm_next / (norm + 1e-06)
    direction_sq = norm_next + 2.0 * ratio * (norm - step * curvature) + ratio * ratio * norm
    return step, norm_next, ratio, direction_sq


def middle_kernel(own_sums, got_sums, right_side, image, *refs):
    k_refs, (residual, direction, partial, partial_low) = refs[:-4], refs[-4:]
    step, _, ratio, _ = scalars(own_sums, got_sums)
    first = right_side[...]
    res = first - step * image[...]
    new = res + ratio * first
    residual[...] = res
    direction[...] = new

    def emit(cols, value):
        partial[:, cols] = value
        partial_low[:, cols] = value.astype(BF16)

    times_kernel(new.astype(BF16), k_refs, emit)


def last_kernel(rows, own_sums, got_sums, low, own, got, right_side, residual, direction, *out):
    step, norm_next, _, direction_sq = scalars(own_sums, got_sums)
    wide = own.shape[1]
    squares = low[:, wide:].astype(F32) + got[:, wide:].astype(F32)
    curvature = jnp.sum(squares, axis=1, keepdims=True) * (1.0 / rows) + 0.5 * direction_sq
    step_two = norm_next / (curvature + 1e-06)
    new = direction[...]
    image = (own[...] + got[:, :wide].astype(F32)) * (1.0 / rows) + 0.5 * new
    coef = (step * right_side[...] + step_two * new).astype(BF16)
    res = (residual[...] - step_two * image).astype(BF16)
    w = coef.shape[0]
    width = out[0].shape[1]
    half = width // CORES
    cut = half // CHUNKS
    for first, value in ((0, coef), (w, res)):
        rows = slice(first, first + w)
        out[0][rows, :] = value[:, :width]
        for index, (hop, far, chunk) in enumerate(segments()):
            at, to = width + index * cut, far * half + chunk * cut
            out[hop][rows, to : to + cut] = value[:, at : at + cut]


def place_kernel(w, place, *refs):
    mine, other = refs[:QUAD], refs[QUAD : 2 * QUAD]
    coef, residual, coef_t, residual_t = refs[2 * QUAD :]
    core, quad = place[0], place[1]
    half = coef.shape[0] // CORES
    for hop in range(QUAD):
        group = jnp.bitwise_xor(quad, hop) * CORES
        for swapped, piece, at in ((0, mine[hop], group + core), (1, other[hop], group + 1 - core)):
            rows = pl.ds(pl.multiple_of(at * w, w), w)
            for index in range(CORES):
                to = index if hop == 0 else jnp.bitwise_xor(core, index ^ swapped)
                cols = pl.ds(pl.multiple_of(to * half, half), half)
                source = slice(index * half, (index + 1) * half)
                coef_t[rows, cols] = piece[0:w, source]
                residual_t[rows, cols] = piece[w : 2 * w, source]
    coef[...] = coef_t[...].T.astype(F32)
    residual[...] = residual_t[...].T.astype(F32)


def run(copies):
    for copy in copies:
        copy.start()
    for copy in copies:
        copy.wait()


def split_kernel(centers, *refs):
    chunks, sems = refs[:-1], refs[-1]
    cut = chunks[0].shape[0]
    at = (lax.axis_index("dp") % CORES) * (cut * CHUNKS)
    run(
        [
            pltpu.make_async_copy(centers.at[pl.ds(pl.multiple_of(at + k * cut, cut), cut), :], chunk, sems.at[k])
            for k, chunk in enumerate(chunks)
        ]
    )


def keep_kernel(value, out, sem):
    run([pltpu.make_async_copy(value, out, sem)])


def fork_kernel(y, z, both, send, sems):
    cut = y.shape[0]
    copies = [
        pltpu.make_async_copy(y, both.at[pl.ds(0, cut), :], sems.at[0]),
        pltpu.make_async_copy(z, both.at[pl.ds(cut, cut), :], sems.at[1]),
    ]
    for copy in copies:
        copy.start()
    core = lax.axis_index("dp") % CORES

    @pl.when(core == 0)
    def _():
        run([pltpu.make_async_copy(z, send, sems.at[2])])

    @pl.when(core != 0)
    def _():
        run([pltpu.make_async_copy(y, send, sems.at[2])])

    for copy in copies:
        copy.wait()


def join_kernel(a, b, both, sems):
    cut = a.shape[0]
    run(
        [
            pltpu.make_async_copy(a, both.at[pl.ds(0, cut), :], sems.at[0]),
            pltpu.make_async_copy(b, both.at[pl.ds(cut, cut), :], sems.at[1]),
        ]
    )


def on_device(features, centers, targets):
    n_dp, n_center = lax.axis_size("dp"), lax.axis_size("center")
    chips, halves = n_dp // CORES, n_center // QUAD
    dp_at, center_at = lax.axis_index("dp"), lax.axis_index("center")
    core, quad = dp_at % CORES, center_at % QUAD
    examples, columns, block = features.shape[0], targets.shape[1], centers.shape[0]
    total_rows = examples * n_dp
    w = columns // (QUAD * CORES)
    half = block // CORES

    def swap(value):
        return lax.ppermute(value, "dp", [(i, i ^ 1) for i in range(n_dp)])

    def over_quad(value, hop):
        return lax.ppermute(value, "center", [(j, j ^ hop) for j in range(n_center)])

    def others(value, axis, size, inner):
        n = size * inner
        got = None
        for shift in range(1, size):
            pairs = [(i, (i // inner + shift) % size * inner + i % inner) for i in range(n)]
            piece = lax.ppermute(value, axis, pairs)
            got = piece if got is None else got.astype(F32) + piece.astype(F32)
        return got

    def over_x(value):
        return others(value, "dp", chips, CORES)

    def over_halves(value):
        return others(value, "center", halves, QUAD)

    sd = jax.ShapeDtypeStruct
    place = jnp.stack([core, quad]).astype(jnp.int32)
    depth = centers.shape[1]
    mine_size = half * depth
    any_space = pl.BlockSpec(memory_space=pl.ANY)
    cut = half // CHUNKS
    chunks = vmem_call(
        split_kernel,
        [sd((cut, depth), BF16)] * CHUNKS,
        [pltpu.SemaphoreType.DMA((CHUNKS,))],
        flops=1000000,
        limit=(64 << 20) - 2 * (mine_size + targets.size) - (1 << 19),
        in_specs=[any_space],
    )(centers)
    y_in, z_in = [], []
    for k in range(CHUNKS):
        y_in.append(over_quad(chunks[k], 1))
        z_in.append(over_quad(chunks[k], 2))
    features_two = swap(features)
    features_two, = vmem_call(
        keep_kernel,
        [pltpu.VMEM(features.shape, BF16)],
        [pltpu.SemaphoreType.DMA(())],
        flops=1000000,
        in_specs=[any_space],
    )(features_two)

    row = lax.broadcasted_iota(jnp.int32, (CORES * QUAD * w, columns), 0)
    group = (quad ^ (row // w % QUAD)) * CORES + (core ^ (row // (QUAD * w)))
    chosen = (group * w + row % w == lax.broadcasted_iota(jnp.int32, row.shape, 1)).astype(BF16)
    wanted = lax.dot_general(chosen, targets, NT, preferred_element_type=F32).astype(BF16)
    wanted_two = swap(wanted[QUAD * w :])
    wanted = wanted[: QUAD * w]

    def build(rows):
        return kernel_block(features, rows), kernel_block(features_two, rows)

    own = build(centers)
    wide = QUAD * block
    flops = 2 * 256 * CORES * examples * wide
    side, = vmem_call(side_kernel, [sd((QUAD * w, block), F32)], flops=flops // 4)(
        wanted, wanted_two, *own
    )
    got_side = over_x(side)
    pairs = []
    for i in range(n_dp):
        hop = 1 if i % CORES == 0 else 2
        pairs += [(i * n_center + j, i * n_center + (j ^ hop)) for j in range(n_center)]
    early_groups, d_in = [own], []
    for k in range(CHUNKS):
        near, d_send = vmem_call(
            fork_kernel,
            [pltpu.VMEM((2 * cut, depth), BF16), pltpu.VMEM((cut, depth), BF16)],
            [pltpu.SemaphoreType.DMA((3,))],
            flops=1000000,
            in_specs=[any_space] * 2,
        )(y_in[k], z_in[k])
        d_in.append(lax.ppermute(d_send, ("dp", "center"), pairs))
        far = swap(near)
        early_groups.append(build(near))
        early_groups.append(build(far))
    sides = vmem_call(
        functools.partial(right_kernel, 1.0 / math.sqrt(total_rows)), [sd((w, block), F32)] * QUAD, flops=1000000
    )(side, got_side)
    sides = [sides[0]] + [over_quad(sides[hop], hop) for hop in range(1, QUAD)]
    early_pieces = [p[0] for p in early_groups]
    d_near = d_in[0]
    if CHUNKS > 1:
        d_near, = vmem_call(
            join_kernel,
            [pltpu.VMEM((half, depth), BF16)],
            [pltpu.SemaphoreType.DMA((CHUNKS,))],
            flops=1000000,
            in_specs=[any_space] * CHUNKS,
        )(*d_in)
    d_far = swap(d_near)
    d_0, d_1 = build(d_near), build(d_far)
    late_pieces = [d_0[0], d_1[0]]
    part = sd((w, examples), F32), sd((w, examples), BF16)
    right_side, low_last, early = vmem_call(
        functools.partial(early_kernel, len(early_pieces), wide - block),
        [sd((w, wide), F32), sd((w, block), BF16), part[0]],
        flops=flops * 3 // 8,
    )(*sides, *early_pieces)
    one = early_pieces + late_pieces
    two = [p[1] for p in early_groups] + [d_0[1], d_1[1]]
    partial, low = vmem_call(late_kernel, part, flops=flops // 8)(low_last, early, *late_pieces)
    got = over_halves(low)
    partial_two, low_two = vmem_call(second_kernel, part, flops=flops // 2)(right_side, *two)
    got_two = over_halves(low_two)
    image_shape, sums_shape = sd((w, wide), F32), sd((w, LANES), F32)
    image, _ = vmem_call(back_kernel, [image_shape, sums_shape], flops=flops // 2)(partial, got, *one)
    image, = vmem_call(back_rest_kernel, [image_shape], flops=flops // 2)(partial_two, got_two, image, *two)
    got = over_x(image)
    image, dots = vmem_call(functools.partial(sums_kernel, total_rows), [image_shape, sums_shape], flops=1000000)(
        image, got, right_side
    )
    got_dots = over_halves(dots)
    residual, direction, partial, low = vmem_call(
        middle_kernel, [image_shape, image_shape, *part], flops=flops // 2
    )(dots, got_dots, right_side, image, *one)
    got = over_halves(low)
    partial_two, low_two = vmem_call(second_kernel, part, flops=flops // 2)(direction, *two)
    got_two = over_halves(low_two)
    image, squares = vmem_call(back_kernel, [image_shape, sums_shape], flops=flops // 2)(partial, got, *one)
    image, image_low = vmem_call(
        back_last_kernel, [image_shape, sd((w, wide + LANES), BF16)], flops=flops // 2
    )(partial_two, got_two, image, squares, *two)
    got = over_x(image_low)
    finals = vmem_call(
        functools.partial(last_kernel, total_rows), [sd((2 * w, block), BF16)] * QUAD, flops=1000000
    )(dots, got_dots, image_low, image, got, right_side, residual, direction)
    landed = [finals[0]]
    for hop in range(1, QUAD):
        landed.append(over_quad(finals[hop], hop))
    landed_two = [swap(piece) for piece in landed]
    return tuple(
        vmem_call(
            functools.partial(place_kernel, w),
            [sd((block, columns), F32)] * 2,
            [pltpu.VMEM((columns, block), BF16)] * 2,
            flops=1000000,
            in_specs=[pl.BlockSpec(memory_space=pltpu.SMEM)] + [pl.BlockSpec(memory_space=pltpu.VMEM)] * (2 * QUAD),
        )(place, *landed, *landed_two)
    )


def solution(mesh):
    placed = (P("dp", None), P("center", None), P("dp", None))
    return jax.shard_map(
        on_device,
        mesh=mesh,
        in_specs=placed,
        out_specs=(P("center", None), P("center", None)),
        check_vma=False,
    )
```

profile of v0, /device:TPU:0, one launch (start us, length us, event | category | flops | bytes accessed | tf_op | source)
XLA Modules:
  0.0 101.1 jit_solution(14134795284906317256)
XLA Ops:
  0.6 1.9 %shard_map.53 = (bf16[128,1024]{1,0:T(8,128)(2,1)}, bf16[128,1024]{1,0:T(8,128)(2,1)}) custom-call(bf16[512,1024]{1,0:T(8,128)(2,1)} %centers.1), custom_call_target="tpu_custom_call" | custom-call | flops 1000000 | tf_op jit(solution)/shard_map/pallas_call | solution.py:345
  2.6 3.1 %collective-permute-start.6 = (bf16[128,1024]{1,0:T(8,128)(2,1)}, bf16[128,1024]{1,0:T(8,128)(2,1)S(1)}, u32[]{:S(2)}, u32[]{:S(2)}) collective-permute-start(bf16[128,1024]{1,0:T(8,128)(2,1)} %get-tuple-element.40), channel_id=1, source_target_pairs={{0,1},{1,0},{2,3},{3,2},{4,5},{5,4},{6,7},{7,6},{8,9},{9,8},{10,11... | collective-permute-start | bytes 786440 | tf_op jit(solution)/shard_map/ppermute | solution.py:322
  5.6 1.6 %collective-permute-start.7 = (bf16[128,1024]{1,0:T(8,128)(2,1)}, bf16[128,1024]{1,0:T(8,128)(2,1)S(1)}, u32[]{:S(2)}, u32[]{:S(2)}) collective-permute-start(bf16[128,1024]{1,0:T(8,128)(2,1)} %get-tuple-element.40), channel_id=1, source_target_pairs={{0,2},{1,3},{2,0},{3,1},{4,6},{5,7},{6,4},{7,5},{8,10},{9,11},{10,... | collective-permute-start | bytes 786440 | tf_op jit(solution)/shard_map/ppermute | solution.py:322
  7.2 0.5 collective-permute-start.9
  7.8 3.2 %fusion.one.refs_4_.refs_0_ = bf16[1024,512]{1,0:T(8,128)(2,1)S(1)} fusion(bf16[1024,1024]{1,0:T(8,128)(2,1)} %param.3, bf16[512,1024]{1,0:T(8,128)(2,1)} %centers.1), kind=kOutput, calls=%fused_computation.2 | convolution fusion | flops 1076363264 | bytes 4194304 | tf_op jit(solution)/shard_map/dot_general | solution.py:38
  11.0 1.0 convolution_convert_fusion
  12.1 0.9 collective-permute-done.6.y
  13.0 2.0 %collective-permute-done.7.z = bf16[128,1024]{1,0:T(8,128)(2,1)S(1)} collective-permute-done((bf16[128,1024]{1,0:T(8,128)(2,1)}, bf16[128,1024]{1,0:T(8,128)(2,1)S(1)}, u32[]{:S(2)}, u32[]{:S(2)}) %collective-permute-start.7) | collective-permute-done | bytes 262176 | tf_op jit(solution)/shard_map/ppermute | solution.py:322
  15.2 2.6 %collective-permute-done.9.y = bf16[128,1024]{1,0:T(8,128)(2,1)S(1)} collective-permute-done((bf16[128,1024]{1,0:T(8,128)(2,1)}, bf16[128,1024]{1,0:T(8,128)(2,1)S(1)}, u32[]{:S(2)}, u32[]{:S(2)}) %collective-permute-start.9) | collective-permute-done | bytes 262176 | tf_op jit(solution)/shard_map/ppermute | solution.py:322
  17.8 1.7 %collective-permute-start.12 = (bf16[128,1024]{1,0:T(8,128)(2,1)S(1)}, bf16[128,1024]{1,0:T(8,128)(2,1)S(1)}, u32[]{:S(2)}, u32[]{:S(2)}) collective-permute-start(bf16[128,1024]{1,0:T(8,128)(2,1)S(1)} %get-tuple-element.45), channel_id=1, source_target_pairs={{0,1},{1,0},{2,3},{3,2},{4,5},{5,4},{6,7},{7,6},{8,10},{9,11},{10,... | collective-permute-start | bytes 786440 | tf_op jit(solution)/shard_map/ppermute | solution.py:396
  19.6 0.4 collective-permute-start.13
  20.0 0.7 fusion.26.refs_5_.refs_1_
  20.7 0.8 fusion.28.refs_7_.refs_3_
  21.5 2.7 %collective-permute-done.12.a = bf16[128,1024]{1,0:T(8,128)(2,1)S(1)} collective-permute-done((bf16[128,1024]{1,0:T(8,128)(2,1)S(1)}, bf16[128,1024]{1,0:T(8,128)(2,1)S(1)}, u32[]{:S(2)}, u32[]{:S(2)}) %collective-permute-start.12) | collective-permute-done | bytes 262176 | tf_op jit(solution)/shard_map/ppermute | solution.py:396
  24.1 2.8 %collective-permute-done.13.b = bf16[128,1024]{1,0:T(8,128)(2,1)S(1)} collective-permute-done((bf16[128,1024]{1,0:T(8,128)(2,1)S(1)}, bf16[128,1024]{1,0:T(8,128)(2,1)S(1)}, u32[]{:S(2)}, u32[]{:S(2)}) %collective-permute-start.13) | collective-permute-done | bytes 262176 | tf_op jit(solution)/shard_map/ppermute | solution.py:396
  26.9 0.2 shard_map.57
  27.3 0.7 fusion.36.refs_0_.refs_5_
  28.0 0.7 fusion.27.refs_6_.refs_2_
  28.8 0.7 fusion.29.refs_8_.refs_4_
  29.6 0.7 fusion.37.refs_1_.refs_6_
  30.3 1.7 %shard_map.50 = bf16[1024,1024]{1,0:T(8,128)(2,1)S(1)} custom-call(bf16[1024,1024]{1,0:T(8,128)(2,1)} %collective-permute-done.1.value), custom_call_target="tpu_custom_call" | custom-call | flops 1000000 | tf_op jit(solution)/shard_map/pallas_call | solution.py:358
  32.2 1.3 %fusion.1.two.refs_0_ = bf16[1024,512]{1,0:T(8,128)(2,1)S(1)} fusion(bf16[1024,1024]{1,0:T(8,128)(2,1)S(1)} %shard_map.50, bf16[512,1024]{1,0:T(8,128)(2,1)S(1)} %copy-done.1), kind=kOutput, calls=%fused_computation.3 | convolution fusion | flops 1076363264 | bytes 4194304 | tf_op jit(solution)/shard_map/dot_general | solution.py:38
  33.5 0.7 fusion.30.refs_1_
  34.3 0.8 fusion.32.refs_3_
  35.0 0.8 fusion.34.refs_5_
  35.8 0.4 shard_map.51.own
  36.2 1.8 %collective-permute-start.2 = (f32[128,512]{1,0:T(8,128)S(1)}, f32[128,512]{1,0:T(8,128)S(1)}, u32[]{:S(2)}, u32[]{:S(2)}) collective-permute-start(f32[128,512]{1,0:T(8,128)S(1)} %shard_map.51.own), channel_id=1, source_target_pairs={{0,16},{8,24},{16,0},{24,8},{1,17},{9,25},{17,1},{25,9},{2,18},{10... | collective-permute-start | bytes 786440 | tf_op jit(solution)/shard_map/ppermute | solution.py:329
  38.0 0.7 fusion.31.refs_2_
  38.8 0.8 fusion.33.refs_4_
  39.5 5.5 %collective-permute-done.2.got = f32[128,512]{1,0:T(8,128)S(1)} collective-permute-done((f32[128,512]{1,0:T(8,128)S(1)}, f32[128,512]{1,0:T(8,128)S(1)}, u32[]{:S(2)}, u32[]{:S(2)}) %collective-permute-start.2) | collective-permute-done | bytes 262176 | tf_op jit(solution)/shard_map/ppermute | solution.py:329
  45.0 1.8 %collective-permute-start.3 = (f32[32,512]{1,0:T(8,128)S(1)}, f32[32,512]{1,0:T(8,128)S(1)}, u32[]{:S(2)}, u32[]{:S(2)}) collective-permute-start(f32[32,512]{1,0:T(8,128)S(1)} %get-tuple-element.37), channel_id=1, source_target_pairs={{0,1},{1,0},{2,3},{3,2},{4,5},{5,4},{6,7},{7,6},{8,9},{9,8},{10,11... | collective-permute-start | bytes 196616 | tf_op jit(solution)/shard_map/ppermute | solution.py:322
  46.9 1.6 %collective-permute-start.4 = (f32[32,512]{1,0:T(8,128)S(1)}, f32[32,512]{1,0:T(8,128)S(1)}, u32[]{:S(2)}, u32[]{:S(2)}) collective-permute-start(f32[32,512]{1,0:T(8,128)S(1)} %get-tuple-element.38), channel_id=1, source_target_pairs={{0,2},{1,3},{2,0},{3,1},{4,6},{5,7},{6,4},{7,5},{8,10},{9,11},{10,... | collective-permute-start | bytes 196616 | tf_op jit(solution)/shard_map/ppermute | solution.py:322
  48.6 0.7 fusion.35.refs_6_
  49.4 2.1 %collective-permute-done.4.refs_2_ = f32[32,512]{1,0:T(8,128)S(1)} collective-permute-done((f32[32,512]{1,0:T(8,128)S(1)}, f32[32,512]{1,0:T(8,128)S(1)}, u32[]{:S(2)}, u32[]{:S(2)}) %collective-permute-start.4) | collective-permute-done | bytes 65568 | tf_op jit(solution)/shard_map/ppermute | solution.py:322
  51.5 2.1 %collective-permute-done.5.refs_3_ = f32[32,512]{1,0:T(8,128)S(1)} collective-permute-done((f32[32,512]{1,0:T(8,128)S(1)}, f32[32,512]{1,0:T(8,128)S(1)}, u32[]{:S(2)}, u32[]{:S(2)}) %collective-permute-start.5) | collective-permute-done | bytes 65568 | tf_op jit(solution)/shard_map/ppermute | solution.py:322
  53.6 1.0 %shard_map.56 = (f32[32,2048]{1,0:T(8,128)S(1)}, bf16[32,512]{1,0:T(8,128)(2,1)S(1)}, f32[32,1024]{1,0:T(8,128)S(1)}) custom-call(f32[32,512]{1,0:T(8,128)S(1)} %get-tuple-element.36.refs_0_, f32[32,512]{1,0:T(8,128)S(1)} %collective-permute-done.3.refs_1_, f32[32,512]{1,0:T(8,128)S(1)} %collective-permute-done.4.refs_2_, ...), custom_call_target="tpu_custom_call" | custom-call | flops 805306368 | tf_op jit(solution)/shard_map/pallas_call | solution.py:418
  54.6 0.5 shard_map.59
  55.1 2.6 %collective-permute-start.16 = (bf16[32,1024]{1,0:T(8,128)(2,1)S(1)}, bf16[32,1024]{1,0:T(8,128)(2,1)S(1)}, u32[]{:S(2)}, u32[]{:S(2)}) collective-permute-start(bf16[32,1024]{1,0:T(8,128)(2,1)S(1)} %get-tuple-element.52), channel_id=1, source_target_pairs={{0,4},{1,5},{2,6},{3,7},{4,0},{5,1},{6,2},{7,3},{8,12},{9,13},{10,... | collective-permute-start | bytes 196616 | tf_op jit(solution)/shard_map/ppermute | solution.py:329
  57.7 1.3 %shard_map.58 = (f32[32,1024]{1,0:T(8,128)S(1)}, bf16[32,1024]{1,0:T(8,128)(2,1)S(1)}) custom-call(f32[32,2048]{1,0:T(8,128)S(1)} %get-tuple-element.44.direction.right_side, bf16[1024,512]{1,0:T(8,128)(2,1)S(1)} %fusion.1.two.refs_0_, bf16[1024,256]{1,0:T(8,128)(2,1)S(1)} %fusion.30.refs_1_, bf16[1024,256]{1,0:T(8,128)(2,1)S(1)} %fusion.31.refs_2_, ...), custom_call_target="tpu_custom_call" | custom-call | flops 1073741824 | tf_op jit(solution)/shard_map/pallas_call | solution.py:427
  59.0 0.4 collective-permute-start.15
  59.4 2.8 %collective-permute-done.16.got = bf16[32,1024]{1,0:T(8,128)(2,1)S(1)} collective-permute-done((bf16[32,1024]{1,0:T(8,128)(2,1)S(1)}, bf16[32,1024]{1,0:T(8,128)(2,1)S(1)}, u32[]{:S(2)}, u32[]{:S(2)}) %collective-permute-start.16) | collective-permute-done | bytes 65568 | tf_op jit(solution)/shard_map/ppermute | solution.py:329
  62.3 1.3 %shard_map.60 = (f32[32,2048]{1,0:T(8,128)S(1)}, f32[32,128]{1,0:T(8,128)}) custom-call(f32[32,1024]{1,0:T(8,128)S(1)} %get-tuple-element.51.partial, bf16[32,1024]{1,0:T(8,128)(2,1)S(1)} %collective-permute-done.16.got, bf16[1024,512]{1,0:T(8,128)(2,1)S(1)} %fusion.one.refs_4_.refs_0_, bf16[1024,256]{1,0:T(8,128)(2,1)S(1)} %fusion.26.refs_5_.refs_1_, ...), custom_call_target="tpu_custom_call" | custom-call | flops 1073741824 | tf_op jit(solution)/shard_map/pallas_call | solution.py:430
  63.6 1.3 %collective-permute-done.15.got = bf16[32,1024]{1,0:T(8,128)(2,1)S(1)} collective-permute-done((bf16[32,1024]{1,0:T(8,128)(2,1)S(1)}, bf16[32,1024]{1,0:T(8,128)(2,1)S(1)}, u32[]{:S(2)}, u32[]{:S(2)}) %collective-permute-start.15) | collective-permute-done | bytes 65568 | tf_op jit(solution)/shard_map/ppermute | solution.py:329
  64.9 0.8 shard_map.61.own
  65.7 1.5 %collective-permute-start.17 = (f32[32,2048]{1,0:T(8,128)S(1)}, f32[32,2048]{1,0:T(8,128)S(1)}, u32[]{:S(2)}, u32[]{:S(2)}) collective-permute-start(f32[32,2048]{1,0:T(8,128)S(1)} %shard_map.61.own), channel_id=1, source_target_pairs={{0,16},{8,24},{16,0},{24,8},{1,17},{9,25},{17,1},{25,9},{2,18},{10... | collective-permute-start | bytes 786440 | tf_op jit(solution)/shard_map/ppermute | solution.py:329
  67.2 4.9 %collective-permute-done.17.got = f32[32,2048]{1,0:T(8,128)S(1)} collective-permute-done((f32[32,2048]{1,0:T(8,128)S(1)}, f32[32,2048]{1,0:T(8,128)S(1)}, u32[]{:S(2)}, u32[]{:S(2)}) %collective-permute-start.17) | collective-permute-done | bytes 262176 | tf_op jit(solution)/shard_map/ppermute | solution.py:329
  72.3 4.6 %collective-permute-done.18.got_sums = f32[32,128]{1,0:T(8,128)S(1)} collective-permute-done((f32[32,128]{1,0:T(8,128)S(1)}, f32[32,128]{1,0:T(8,128)S(1)}, u32[]{:S(2)}, u32[]{:S(2)}) %collective-permute-start.18) | collective-permute-done | bytes 16416 | tf_op jit(solution)/shard_map/ppermute | solution.py:329
  76.9 1.4 %shard_map.63 = (f32[32,2048]{1,0:T(8,128)S(1)}, f32[32,2048]{1,0:T(8,128)S(1)}, f32[32,1024]{1,0:T(8,128)S(1)}, bf16[32,1024]{1,0:T(8,128)(2,1)S(1)}) custom-call(f32[32,128]{1,0:T(8,128)S(1)} %get-tuple-element.54.own_sums, f32[32,128]{1,0:T(8,128)S(1)} %collective-permute-done.18.got_sums, f32[32,2048]{1,0:T(8,128)S(1)} %get-tuple-element.44.direction.right_side, ...), custom_call_target="tpu_custom_call" | custom-call | flops 1073741824 | tf_op jit(solution)/shard_map/pallas_call | solution.py:437
  78.4 1.3 %shard_map.64 = (f32[32,1024]{1,0:T(8,128)S(1)}, bf16[32,1024]{1,0:T(8,128)(2,1)S(1)}) custom-call(f32[32,2048]{1,0:T(8,128)S(1)} %get-tuple-element.56.direction, bf16[1024,512]{1,0:T(8,128)(2,1)S(1)} %fusion.1.two.refs_0_, bf16[1024,256]{1,0:T(8,128)(2,1)S(1)} %fusion.30.refs_1_, bf16[1024,256]{1,0:T(8,128)(2,1)S(1)} %fusion.31.refs_2_, ...), custom_call_target="tpu_custom_call" | custom-call | flops 1073741824 | tf_op jit(solution)/shard_map/pallas_call | solution.py:441
  79.7 3.0 %collective-permute-start.19 = (bf16[32,1024]{1,0:T(8,128)(2,1)S(1)}, bf16[32,1024]{1,0:T(8,128)(2,1)S(1)}, u32[]{:S(2)}, u32[]{:S(2)}) collective-permute-start(bf16[32,1024]{1,0:T(8,128)(2,1)S(1)} %get-tuple-element.58), channel_id=1, source_target_pairs={{0,4},{1,5},{2,6},{3,7},{4,0},{5,1},{6,2},{7,3},{8,12},{9,13},{10,... | collective-permute-start | bytes 196616 | tf_op jit(solution)/shard_map/ppermute | solution.py:329
  82.7 1.1 %collective-permute-done.20.got = bf16[32,1024]{1,0:T(8,128)(2,1)S(1)} collective-permute-done((bf16[32,1024]{1,0:T(8,128)(2,1)S(1)}, bf16[32,1024]{1,0:T(8,128)(2,1)S(1)}, u32[]{:S(2)}, u32[]{:S(2)}) %collective-permute-start.20) | collective-permute-done | bytes 65568 | tf_op jit(solution)/shard_map/ppermute | solution.py:329
  83.8 0.8 shard_map.65
  84.6 0.8 collective-permute-done.19.got
  85.4 0.8 shard_map.66
  86.3 1.6 %collective-permute-start.21 = (bf16[32,2176]{1,0:T(8,128)(2,1)S(1)}, bf16[32,2176]{1,0:T(8,128)(2,1)S(1)}, u32[]{:S(2)}, u32[]{:S(2)}) collective-permute-start(bf16[32,2176]{1,0:T(8,128)(2,1)S(1)} %get-tuple-element.63.low), channel_id=1, source_target_pairs={{0,16},{8,24},{16,0},{24,8},{1,17},{9,25},{17,1},{25,9},{2,18},{10... | collective-permute-start | bytes 417800 | tf_op jit(solution)/shard_map/ppermute | solution.py:329
  87.8 3.6 %collective-permute-done.21.got = bf16[32,2176]{1,0:T(8,128)(2,1)S(1)} collective-permute-done((bf16[32,2176]{1,0:T(8,128)(2,1)S(1)}, bf16[32,2176]{1,0:T(8,128)(2,1)S(1)}, u32[]{:S(2)}, u32[]{:S(2)}) %collective-permute-start.21) | collective-permute-done | bytes 139296 | tf_op jit(solution)/shard_map/ppermute | solution.py:329
  91.4 0.2 shard_map.67
  91.6 1.1 %collective-permute-start.22 = (bf16[64,512]{1,0:T(8,128)(2,1)S(1)}, bf16[64,512]{1,0:T(8,128)(2,1)S(1)}, u32[]{:S(2)}, u32[]{:S(2)}) collective-permute-start(bf16[64,512]{1,0:T(8,128)(2,1)S(1)} %get-tuple-element.67), channel_id=1, source_target_pairs={{0,1},{1,0},{2,3},{3,2},{4,5},{5,4},{6,7},{7,6},{8,9},{9,8},{10,11... | collective-permute-start | bytes 196616 | tf_op jit(solution)/shard_map/ppermute | solution.py:322
  92.8 2.4 %collective-permute-start.24 = (bf16[64,512]{1,0:T(8,128)(2,1)S(1)}, bf16[64,512]{1,0:T(8,128)(2,1)S(1)}, u32[]{:S(2)}, u32[]{:S(2)}) collective-permute-start(bf16[64,512]{1,0:T(8,128)(2,1)S(1)} %get-tuple-element.69), channel_id=1, source_target_pairs={{0,3},{1,2},{2,1},{3,0},{4,7},{5,6},{6,5},{7,4},{8,11},{9,10},{10,... | collective-permute-start | bytes 196616 | tf_op jit(solution)/shard_map/ppermute | solution.py:322
  95.2 0.8 collective-permute-done.22.refs_1_
  96.0 1.0 collective-permute-done.23.refs_2_
  97.0 1.2 %collective-permute-done.24.refs_3_ = bf16[64,512]{1,0:T(8,128)(2,1)S(1)} collective-permute-done((bf16[64,512]{1,0:T(8,128)(2,1)S(1)}, bf16[64,512]{1,0:T(8,128)(2,1)S(1)}, u32[]{:S(2)}, u32[]{:S(2)}) %collective-permute-start.24) | collective-permute-done | bytes 65568 | tf_op jit(solution)/shard_map/ppermute | solution.py:322
  98.2 1.2 %collective-permute-done.28.refs_7_ = bf16[64,512]{1,0:T(8,128)(2,1)S(1)} collective-permute-done((bf16[64,512]{1,0:T(8,128)(2,1)S(1)}, bf16[64,512]{1,0:T(8,128)(2,1)S(1)}, u32[]{:S(2)}, u32[]{:S(2)}) %collective-permute-start.28) | collective-permute-done | bytes 65568 | tf_op jit(solution)/shard_map/ppermute | solution.py:319
  99.4 1.7 %shard_map.68 = (f32[512,256]{1,0:T(8,128)}, f32[512,256]{1,0:T(8,128)}) custom-call(s32[2]{0:T(128)S(1)} %pad_add_fusion.place, bf16[64,512]{1,0:T(8,128)(2,1)S(1)} %get-tuple-element.66.refs_0_, bf16[64,512]{1,0:T(8,128)(2,1)S(1)} %collective-permute-done.22.refs_1_, bf16[64,512]{1,0:T(8,128)(2,1)S(1)} %collective-permute-done.23.refs_2_, ...), custom_call_target="tpu_custom_call" | custom-call | flops 1000000 | tf_op jit(solution)/shard_map/pallas_call | solution.py:456
  (41 shorter events, 1.3 us)
Async XLA Ops:
  0.6 10.4 %copy-start = (bf16[1024,256]{1,0:T(8,128)(2,1)S(1)}, bf16[1024,256]{1,0:T(8,128)(2,1)}, u32[]{:S(2)}) copy-start(bf16[1024,256]{1,0:T(8,128)(2,1)} %param.5) | copy-start | bytes 1572868
  2.6 10.4 %collective-permute-start.6 = (bf16[128,1024]{1,0:T(8,128)(2,1)}, bf16[128,1024]{1,0:T(8,128)(2,1)S(1)}, u32[]{:S(2)}, u32[]{:S(2)}) collective-permute-start(bf16[128,1024]{1,0:T(8,128)(2,1)} %get-tuple-element.40), channel_id=1, source_target_pairs={{0,1},{1,0},{2,3},{3,2},{4,5},{5,4},{6,7},{7,6},{8,9},{9,8},{10,11... | collective-permute-start | bytes 786440 | tf_op jit(solution)/shard_map/ppermute | solution.py:322
  5.6 9.4 %collective-permute-start.7 = (bf16[128,1024]{1,0:T(8,128)(2,1)}, bf16[128,1024]{1,0:T(8,128)(2,1)S(1)}, u32[]{:S(2)}, u32[]{:S(2)}) collective-permute-start(bf16[128,1024]{1,0:T(8,128)(2,1)} %get-tuple-element.40), channel_id=1, source_target_pairs={{0,2},{1,3},{2,0},{3,1},{4,6},{5,7},{6,4},{7,5},{8,10},{9,11},{10,... | collective-permute-start | bytes 786440 | tf_op jit(solution)/shard_map/ppermute | solution.py:322
  7.2 10.6 %collective-permute-start.9 = (bf16[128,1024]{1,0:T(8,128)(2,1)}, bf16[128,1024]{1,0:T(8,128)(2,1)S(1)}, u32[]{:S(2)}, u32[]{:S(2)}) collective-permute-start(bf16[128,1024]{1,0:T(8,128)(2,1)} %get-tuple-element.42), channel_id=1, source_target_pairs={{0,1},{1,0},{2,3},{3,2},{4,5},{5,4},{6,7},{7,6},{8,9},{9,8},{10,11... | collective-permute-start | bytes 786440 | tf_op jit(solution)/shard_map/ppermute | solution.py:322
  7.7 11.8 %collective-permute-start.10 = (bf16[128,1024]{1,0:T(8,128)(2,1)}, bf16[128,1024]{1,0:T(8,128)(2,1)S(1)}, u32[]{:S(2)}, u32[]{:S(2)}) collective-permute-start(bf16[128,1024]{1,0:T(8,128)(2,1)} %get-tuple-element.42), channel_id=1, source_target_pairs={{0,2},{1,3},{2,0},{3,1},{4,6},{5,7},{6,4},{7,5},{8,10},{9,11},{10,... | collective-permute-start | bytes 786440 | tf_op jit(solution)/shard_map/ppermute | solution.py:322
  7.7 22.6 %collective-permute-start.1 = (bf16[1024,1024]{1,0:T(8,128)(2,1)}, bf16[1024,1024]{1,0:T(8,128)(2,1)}, u32[]{:S(2)}, u32[]{:S(2)}) collective-permute-start(bf16[1024,1024]{1,0:T(8,128)(2,1)} %param.3), channel_id=1, source_target_pairs={{0,8},{8,0},{16,24},{24,16},{1,9},{9,1},{17,25},{25,17},{2,10},{10... | collective-permute-start | bytes 6291464 | tf_op jit(solution)/shard_map/ppermute | solution.py:319
  11.0 9.0 %copy-start.2 = (bf16[1024,1024]{1,0:T(8,128)(2,1)S(1)}, bf16[1024,1024]{1,0:T(8,128)(2,1)}, u32[]{:S(2)}) copy-start(bf16[1024,1024]{1,0:T(8,128)(2,1)} %param.3) | copy-start | bytes 6291460
  13.0 22.8 %collective-permute-start = (bf16[128,1024]{1,0:T(8,128)(2,1)S(1)}, bf16[128,1024]{1,0:T(8,128)(2,1)S(1)}, u32[]{:S(2)}, u32[]{:S(2)}) collective-permute-start(bf16[128,1024]{1,0:T(8,128)(2,1)S(1)} %get-tuple-element.70), channel_id=1, source_target_pairs={{0,8},{8,0},{16,24},{24,16},{1,9},{9,1},{17,25},{25,17},{2,10},{10... | collective-permute-start | bytes 786440 | tf_op jit(solution)/shard_map/ppermute | solution.py:319
  15.1 12.9 %collective-permute-start.8 = (bf16[256,1024]{1,0:T(8,128)(2,1)S(1)}, bf16[256,1024]{1,0:T(8,128)(2,1)S(1)}, u32[]{:S(2)}, u32[]{:S(2)}) collective-permute-start(bf16[256,1024]{1,0:T(8,128)(2,1)S(1)} %get-tuple-element.41), channel_id=1, source_target_pairs={{0,8},{8,0},{16,24},{24,16},{1,9},{9,1},{17,25},{25,17},{2,10},{10... | collective-permute-start | bytes 1572872 | tf_op jit(solution)/shard_map/ppermute | solution.py:319
  17.8 6.4 %collective-permute-start.12 = (bf16[128,1024]{1,0:T(8,128)(2,1)S(1)}, bf16[128,1024]{1,0:T(8,128)(2,1)S(1)}, u32[]{:S(2)}, u32[]{:S(2)}) collective-permute-start(bf16[128,1024]{1,0:T(8,128)(2,1)S(1)} %get-tuple-element.45), channel_id=1, source_target_pairs={{0,1},{1,0},{2,3},{3,2},{4,5},{5,4},{6,7},{7,6},{8,10},{9,11},{10,... | collective-permute-start | bytes 786440 | tf_op jit(solution)/shard_map/ppermute | solution.py:396
  19.6 7.3 %collective-permute-start.13 = (bf16[128,1024]{1,0:T(8,128)(2,1)S(1)}, bf16[128,1024]{1,0:T(8,128)(2,1)S(1)}, u32[]{:S(2)}, u32[]{:S(2)}) collective-permute-start(bf16[128,1024]{1,0:T(8,128)(2,1)S(1)} %get-tuple-element.46), channel_id=1, source_target_pairs={{0,1},{1,0},{2,3},{3,2},{4,5},{5,4},{6,7},{7,6},{8,10},{9,11},{10,... | collective-permute-start | bytes 786440 | tf_op jit(solution)/shard_map/ppermute | solution.py:396
  24.1 4.7 %collective-permute-start.11 = (bf16[256,1024]{1,0:T(8,128)(2,1)S(1)}, bf16[256,1024]{1,0:T(8,128)(2,1)S(1)}, u32[]{:S(2)}, u32[]{:S(2)}) collective-permute-start(bf16[256,1024]{1,0:T(8,128)(2,1)S(1)} %get-tuple-element.43), channel_id=1, source_target_pairs={{0,8},{8,0},{16,24},{24,16},{1,9},{9,1},{17,25},{25,17},{2,10},{10... | collective-permute-start | bytes 1572872 | tf_op jit(solution)/shard_map/ppermute | solution.py:319
  27.2 2.4 %collective-permute-start.14 = (bf16[256,1024]{1,0:T(8,128)(2,1)S(1)}, bf16[256,1024]{1,0:T(8,128)(2,1)S(1)}, u32[]{:S(2)}, u32[]{:S(2)}) collective-permute-start(bf16[256,1024]{1,0:T(8,128)(2,1)S(1)} %shard_map.57), channel_id=1, source_target_pairs={{0,8},{8,0},{16,24},{24,16},{1,9},{9,1},{17,25},{25,17},{2,10},{10... | collective-permute-start | bytes 1572872 | tf_op jit(solution)/shard_map/ppermute | solution.py:319
  30.3 1.9 %copy-start.1 = (bf16[512,1024]{1,0:T(8,128)(2,1)S(1)}, bf16[512,1024]{1,0:T(8,128)(2,1)}, u32[]{:S(2)}) copy-start(bf16[512,1024]{1,0:T(8,128)(2,1)} %centers.1) | copy-start | bytes 3145732
  36.2 8.8 %collective-permute-start.2 = (f32[128,512]{1,0:T(8,128)S(1)}, f32[128,512]{1,0:T(8,128)S(1)}, u32[]{:S(2)}, u32[]{:S(2)}) collective-permute-start(f32[128,512]{1,0:T(8,128)S(1)} %shard_map.51.own), channel_id=1, source_target_pairs={{0,16},{8,24},{16,0},{24,8},{1,17},{9,25},{17,1},{25,9},{2,18},{10... | collective-permute-start | bytes 786440 | tf_op jit(solution)/shard_map/ppermute | solution.py:329
  45.0 4.3 %collective-permute-start.3 = (f32[32,512]{1,0:T(8,128)S(1)}, f32[32,512]{1,0:T(8,128)S(1)}, u32[]{:S(2)}, u32[]{:S(2)}) collective-permute-start(f32[32,512]{1,0:T(8,128)S(1)} %get-tuple-element.37), channel_id=1, source_target_pairs={{0,1},{1,0},{2,3},{3,2},{4,5},{5,4},{6,7},{7,6},{8,9},{9,8},{10,11... | collective-permute-start | bytes 196616 | tf_op jit(solution)/shard_map/ppermute | solution.py:322
  46.9 4.6 %collective-permute-start.4 = (f32[32,512]{1,0:T(8,128)S(1)}, f32[32,512]{1,0:T(8,128)S(1)}, u32[]{:S(2)}, u32[]{:S(2)}) collective-permute-start(f32[32,512]{1,0:T(8,128)S(1)} %get-tuple-element.38), channel_id=1, source_target_pairs={{0,2},{1,3},{2,0},{3,1},{4,6},{5,7},{6,4},{7,5},{8,10},{9,11},{10,... | collective-permute-start | bytes 196616 | tf_op jit(solution)/shard_map/ppermute | solution.py:322
  48.4 5.2 %collective-permute-start.5 = (f32[32,512]{1,0:T(8,128)S(1)}, f32[32,512]{1,0:T(8,128)S(1)}, u32[]{:S(2)}, u32[]{:S(2)}) collective-permute-start(f32[32,512]{1,0:T(8,128)S(1)} %get-tuple-element.39), channel_id=1, source_target_pairs={{0,3},{1,2},{2,1},{3,0},{4,7},{5,6},{6,5},{7,4},{8,11},{9,10},{10,... | collective-permute-start | bytes 196616 | tf_op jit(solution)/shard_map/ppermute | solution.py:322
  55.1 7.2 %collective-permute-start.16 = (bf16[32,1024]{1,0:T(8,128)(2,1)S(1)}, bf16[32,1024]{1,0:T(8,128)(2,1)S(1)}, u32[]{:S(2)}, u32[]{:S(2)}) collective-permute-start(bf16[32,1024]{1,0:T(8,128)(2,1)S(1)} %get-tuple-element.52), channel_id=1, source_target_pairs={{0,4},{1,5},{2,6},{3,7},{4,0},{5,1},{6,2},{7,3},{8,12},{9,13},{10,... | collective-permute-start | bytes 196616 | tf_op jit(solution)/shard_map/ppermute | solution.py:329
  59.0 5.8 %collective-permute-start.15 = (bf16[32,1024]{1,0:T(8,128)(2,1)S(1)}, bf16[32,1024]{1,0:T(8,128)(2,1)S(1)}, u32[]{:S(2)}, u32[]{:S(2)}) collective-permute-start(bf16[32,1024]{1,0:T(8,128)(2,1)S(1)} %get-tuple-element.48), channel_id=1, source_target_pairs={{0,4},{1,5},{2,6},{3,7},{4,0},{5,1},{6,2},{7,3},{8,12},{9,13},{10,... | collective-permute-start | bytes 196616 | tf_op jit(solution)/shard_map/ppermute | solution.py:329
  65.7 6.4 %collective-permute-start.17 = (f32[32,2048]{1,0:T(8,128)S(1)}, f32[32,2048]{1,0:T(8,128)S(1)}, u32[]{:S(2)}, u32[]{:S(2)}) collective-permute-start(f32[32,2048]{1,0:T(8,128)S(1)} %shard_map.61.own), channel_id=1, source_target_pairs={{0,16},{8,24},{16,0},{24,8},{1,17},{9,25},{17,1},{25,9},{2,18},{10... | collective-permute-start | bytes 786440 | tf_op jit(solution)/shard_map/ppermute | solution.py:329
  72.2 4.7 %collective-permute-start.18 = (f32[32,128]{1,0:T(8,128)S(1)}, f32[32,128]{1,0:T(8,128)S(1)}, u32[]{:S(2)}, u32[]{:S(2)}) collective-permute-start(f32[32,128]{1,0:T(8,128)S(1)} %get-tuple-element.54.own_sums), channel_id=1, source_target_pairs={{0,4},{1,5},{2,6},{3,7},{4,0},{5,1},{6,2},{7,3},{8,12},{9,13},{10,... | collective-permute-start | bytes 49160 | tf_op jit(solution)/shard_map/ppermute | solution.py:329
  78.4 5.5 %collective-permute-start.20 = (bf16[32,1024]{1,0:T(8,128)(2,1)S(1)}, bf16[32,1024]{1,0:T(8,128)(2,1)S(1)}, u32[]{:S(2)}, u32[]{:S(2)}) collective-permute-start(bf16[32,1024]{1,0:T(8,128)(2,1)S(1)} %get-tuple-element.60), channel_id=1, source_target_pairs={{0,4},{1,5},{2,6},{3,7},{4,0},{5,1},{6,2},{7,3},{8,12},{9,13},{10,... | collective-permute-start | bytes 196616 | tf_op jit(solution)/shard_map/ppermute | solution.py:329
  79.7 5.7 %collective-permute-start.19 = (bf16[32,1024]{1,0:T(8,128)(2,1)S(1)}, bf16[32,1024]{1,0:T(8,128)(2,1)S(1)}, u32[]{:S(2)}, u32[]{:S(2)}) collective-permute-start(bf16[32,1024]{1,0:T(8,128)(2,1)S(1)} %get-tuple-element.58), channel_id=1, source_target_pairs={{0,4},{1,5},{2,6},{3,7},{4,0},{5,1},{6,2},{7,3},{8,12},{9,13},{10,... | collective-permute-start | bytes 196616 | tf_op jit(solution)/shard_map/ppermute | solution.py:329
  86.3 5.1 %collective-permute-start.21 = (bf16[32,2176]{1,0:T(8,128)(2,1)S(1)}, bf16[32,2176]{1,0:T(8,128)(2,1)S(1)}, u32[]{:S(2)}, u32[]{:S(2)}) collective-permute-start(bf16[32,2176]{1,0:T(8,128)(2,1)S(1)} %get-tuple-element.63.low), channel_id=1, source_target_pairs={{0,16},{8,24},{16,0},{24,8},{1,17},{9,25},{17,1},{25,9},{2,18},{10... | collective-permute-start | bytes 417800 | tf_op jit(solution)/shard_map/ppermute | solution.py:329
  91.6 4.3 %collective-permute-start.22 = (bf16[64,512]{1,0:T(8,128)(2,1)S(1)}, bf16[64,512]{1,0:T(8,128)(2,1)S(1)}, u32[]{:S(2)}, u32[]{:S(2)}) collective-permute-start(bf16[64,512]{1,0:T(8,128)(2,1)S(1)} %get-tuple-element.67), channel_id=1, source_target_pairs={{0,1},{1,0},{2,3},{3,2},{4,5},{5,4},{6,7},{7,6},{8,9},{9,8},{10,11... | collective-permute-start | bytes 196616 | tf_op jit(solution)/shard_map/ppermute | solution.py:322
  92.7 4.3 %collective-permute-start.23 = (bf16[64,512]{1,0:T(8,128)(2,1)S(1)}, bf16[64,512]{1,0:T(8,128)(2,1)S(1)}, u32[]{:S(2)}, u32[]{:S(2)}) collective-permute-start(bf16[64,512]{1,0:T(8,128)(2,1)S(1)} %get-tuple-element.68), channel_id=1, source_target_pairs={{0,2},{1,3},{2,0},{3,1},{4,6},{5,7},{6,4},{7,5},{8,10},{9,11},{10,... | collective-permute-start | bytes 196616 | tf_op jit(solution)/shard_map/ppermute | solution.py:322
  92.8 5.3 %collective-permute-start.24 = (bf16[64,512]{1,0:T(8,128)(2,1)S(1)}, bf16[64,512]{1,0:T(8,128)(2,1)S(1)}, u32[]{:S(2)}, u32[]{:S(2)}) collective-permute-start(bf16[64,512]{1,0:T(8,128)(2,1)S(1)} %get-tuple-element.69), channel_id=1, source_target_pairs={{0,3},{1,2},{2,1},{3,0},{4,7},{5,6},{6,5},{7,4},{8,11},{9,10},{10,... | collective-permute-start | bytes 196616 | tf_op jit(solution)/shard_map/ppermute | solution.py:322
  95.2 3.0 %collective-permute-start.25 = (bf16[64,512]{1,0:T(8,128)(2,1)S(1)}, bf16[64,512]{1,0:T(8,128)(2,1)S(1)}, u32[]{:S(2)}, u32[]{:S(2)}) collective-permute-start(bf16[64,512]{1,0:T(8,128)(2,1)S(1)} %get-tuple-element.66.refs_0_), channel_id=1, source_target_pairs={{0,8},{8,0},{16,24},{24,16},{1,9},{9,1},{17,25},{25,17},{2,10},{10... | collective-permute-start | bytes 196616 | tf_op jit(solution)/shard_map/ppermute | solution.py:319
  96.0 2.2 %collective-permute-start.26 = (bf16[64,512]{1,0:T(8,128)(2,1)S(1)}, bf16[64,512]{1,0:T(8,128)(2,1)S(1)}, u32[]{:S(2)}, u32[]{:S(2)}) collective-permute-start(bf16[64,512]{1,0:T(8,128)(2,1)S(1)} %collective-permute-done.22.refs_1_), channel_id=1, source_target_pairs={{0,8},{8,0},{16,24},{24,16},{1,9},{9,1},{17,25},{25,17},{2,10},{10... | collective-permute-start | bytes 196616 | tf_op jit(solution)/shard_map/ppermute | solution.py:319
  97.0 1.3 %collective-permute-start.27 = (bf16[64,512]{1,0:T(8,128)(2,1)S(1)}, bf16[64,512]{1,0:T(8,128)(2,1)S(1)}, u32[]{:S(2)}, u32[]{:S(2)}) collective-permute-start(bf16[64,512]{1,0:T(8,128)(2,1)S(1)} %collective-permute-done.23.refs_2_), channel_id=1, source_target_pairs={{0,8},{8,0},{16,24},{24,16},{1,9},{9,1},{17,25},{25,17},{2,10},{10... | collective-permute-start | bytes 196616 | tf_op jit(solution)/shard_map/ppermute | solution.py:319
  98.1 1.3 %collective-permute-start.28 = (bf16[64,512]{1,0:T(8,128)(2,1)S(1)}, bf16[64,512]{1,0:T(8,128)(2,1)S(1)}, u32[]{:S(2)}, u32[]{:S(2)}) collective-permute-start(bf16[64,512]{1,0:T(8,128)(2,1)S(1)} %collective-permute-done.24.refs_3_), channel_id=1, source_target_pairs={{0,8},{8,0},{16,24},{24,16},{1,9},{9,1},{17,25},{25,17},{2,10},{10... | collective-permute-start | bytes 196616 | tf_op jit(solution)/shard_map/ppermute | solution.py:319
where the time goes:
time: 101 us
  waiting for transfers between devices  43.9 us (43%)
  starting transfers between devices  25.5 us (25%)
  Pallas kernels  15.9 us (16%)
  matrix products  14.5 us (14%)
    ppermute x8, waiting for transfers between devices, others(): piece = lax.ppermute(value, axis, pairs)  24.6 us
    dot_general x14, matrix products, kernel_block(): scores = lax.dot_general(rows, centers, NT, preferred_element_type=F32)  13.5 us
    ppermute x10, waiting for transfers between devices, over_quad(): lax.ppermute(value, 'center', [(j, j ^ hop) for j in range(n_center)])  12.7 us
    ppermute x10, starting transfers between devices, over_quad(): lax.ppermute(value, 'center', [(j, j ^ hop) for j in range(n_center)])  12.3 us
    ppermute x8, starting transfers between devices, others(): piece = lax.ppermute(value, axis, pairs)  11 us
    ppermute x2, waiting for transfers between devices, on_device(): d_in.append(lax.ppermute(d_send, ('dp', 'center'), pairs))  5.46 us
    pallas_call x2, Pallas kernels, on_device(): vmem_call(back_kernel, [image_shape, sums_shape], flops=flops // 2)  2.15 us
    ppermute x2, starting transfers between devices, on_device(): d_in.append(lax.ppermute(d_send, ('dp', 'center'), pairs))  2.09 us
  transfers between devices with their start and end apart: 29, of which 19 were waited for; matrix products, arithmetic and copies ran while one was open for 14% of the time, Pallas kernels for 7%

commit v1 on v0

--- a/solution.py
+++ b/solution.py
@@ -231,10 +231,10 @@
             out[hop][rows, to : to + cut] = value[:, at : at + cut]
 
 
-def place_kernel(w, place, *refs):
+def place_kernel(w, *refs):
     mine, other = refs[:QUAD], refs[QUAD : 2 * QUAD]
     coef, residual, coef_t, residual_t = refs[2 * QUAD :]
-    core, quad = place[0], place[1]
+    core, quad = lax.axis_index("dp") % CORES, lax.axis_index("center") % QUAD
     half = coef.shape[0] // CORES
     for hop in range(QUAD):
         group = jnp.bitwise_xor(quad, hop) * CORES
@@ -337,9 +337,7 @@
         return others(value, "center", halves, QUAD)
 
     sd = jax.ShapeDtypeStruct
-    place = jnp.stack([core, quad]).astype(jnp.int32)
     depth = centers.shape[1]
-    mine_size = half * depth
     any_space = pl.BlockSpec(memory_space=pl.ANY)
     cut = half // CHUNKS
     chunks = vmem_call(
@@ -347,7 +345,7 @@
         [sd((cut, depth), BF16)] * CHUNKS,
         [pltpu.SemaphoreType.DMA((CHUNKS,))],
         flops=1000000,
-        limit=(64 << 20) - 2 * (mine_size + targets.size) - (1 << 19),
+        limit=(64 << 20) - 2 * (half * depth + targets.size) - (1 << 19),
         in_specs=[any_space],
     )(centers)
     y_in, z_in = [], []
@@ -458,8 +456,7 @@
             [sd((block, columns), F32)] * 2,
             [pltpu.VMEM((columns, block), BF16)] * 2,
             flops=1000000,
-            in_specs=[pl.BlockSpec(memory_space=pltpu.SMEM)] + [pl.BlockSpec(memory_space=pltpu.VMEM)] * (2 * QUAD),
-        )(place, *landed, *landed_two)
+        )(*landed, *landed_two)
     )
 
 

time: 101 us -> 101 us (level)
  transfers between devices with their start and end apart: 29 -> 29, of which waited for: 19 -> 20; matrix products, arithmetic and copies ran while one was open for 14% -> 15% of each run, Pallas kernels for 7% -> 7%
where the time goes in v1:
time: 101 us
  waiting for transfers between devices  44 us (44%)
  starting transfers between devices  25.5 us (25%)
  Pallas kernels  15.3 us (15%)
  matrix products  14.5 us (14%)
    ppermute x8, waiting for transfers between devices, others(): piece = lax.ppermute(value, axis, pairs)  24.6 us
    dot_general x14, matrix products, kernel_block(): scores = lax.dot_general(rows, centers, NT, preferred_element_type=F32)  13.5 us
    ppermute x10, waiting for transfers between devices, over_quad(): lax.ppermute(value, 'center', [(j, j ^ hop) for j in range(n_center)])  12.7 us
    ppermute x10, starting transfers between devices, over_quad(): lax.ppermute(value, 'center', [(j, j ^ hop) for j in range(n_center)])  12.3 us
    ppermute x8, starting transfers between devices, others(): piece = lax.ppermute(value, axis, pairs)  11 us
    ppermute x2, waiting for transfers between devices, on_device(): d_in.append(lax.ppermute(d_send, ('dp', 'center'), pairs))  5.46 us
    pallas_call x2, Pallas kernels, on_device(): vmem_call(back_kernel, [image_shape, sums_shape], flops=flops // 2)  2.15 us
    ppermute x2, starting transfers between devices, on_device(): d_in.append(lax.ppermute(d_send, ('dp', 'center'), pairs))  2.09 us
  transfers between devices with their start and end apart: 29, of which 20 were waited for; matrix products, arithmetic and copies ran while one was open for 15% of the time, Pallas kernels for 7%

profile of v1, /device:TPU:0, one launch (start us, length us, event | category | flops | bytes accessed | tf_op | source)
XLA Modules:
  0.0 100.5 jit_solution(15999303912989505908)
XLA Ops:
  0.6 1.9 %shard_map.53 = (bf16[128,1024]{1,0:T(8,128)(2,1)}, bf16[128,1024]{1,0:T(8,128)(2,1)}) custom-call(bf16[512,1024]{1,0:T(8,128)(2,1)} %centers.1), custom_call_target="tpu_custom_call" | custom-call | flops 1000000 | tf_op jit(solution)/shard_map/pallas_call | solution.py:343
  2.6 3.1 %collective-permute-start.6 = (bf16[128,1024]{1,0:T(8,128)(2,1)}, bf16[128,1024]{1,0:T(8,128)(2,1)S(1)}, u32[]{:S(2)}, u32[]{:S(2)}) collective-permute-start(bf16[128,1024]{1,0:T(8,128)(2,1)} %get-tuple-element.40), channel_id=1, source_target_pairs={{0,1},{1,0},{2,3},{3,2},{4,5},{5,4},{6,7},{7,6},{8,9},{9,8},{10,11... | collective-permute-start | bytes 786440 | tf_op jit(solution)/shard_map/ppermute | solution.py:322
  5.6 1.6 %collective-permute-start.7 = (bf16[128,1024]{1,0:T(8,128)(2,1)}, bf16[128,1024]{1,0:T(8,128)(2,1)S(1)}, u32[]{:S(2)}, u32[]{:S(2)}) collective-permute-start(bf16[128,1024]{1,0:T(8,128)(2,1)} %get-tuple-element.40), channel_id=1, source_target_pairs={{0,2},{1,3},{2,0},{3,1},{4,6},{5,7},{6,4},{7,5},{8,10},{9,11},{10,... | collective-permute-start | bytes 786440 | tf_op jit(solution)/shard_map/ppermute | solution.py:322
  7.2 0.5 collective-permute-start.9
  7.8 3.2 %fusion.one.refs_4_.refs_0_ = bf16[1024,512]{1,0:T(8,128)(2,1)S(1)} fusion(bf16[1024,1024]{1,0:T(8,128)(2,1)} %param.3, bf16[512,1024]{1,0:T(8,128)(2,1)} %centers.1), kind=kOutput, calls=%fused_computation.2 | convolution fusion | flops 1076363264 | bytes 4194304 | tf_op jit(solution)/shard_map/dot_general | solution.py:38
  11.0 1.0 convolution_convert_fusion
  12.1 0.9 collective-permute-done.6.y
  13.0 2.0 %collective-permute-done.7.z = bf16[128,1024]{1,0:T(8,128)(2,1)S(1)} collective-permute-done((bf16[128,1024]{1,0:T(8,128)(2,1)}, bf16[128,1024]{1,0:T(8,128)(2,1)S(1)}, u32[]{:S(2)}, u32[]{:S(2)}) %collective-permute-start.7) | collective-permute-done | bytes 262176 | tf_op jit(solution)/shard_map/ppermute | solution.py:322
  15.2 2.6 %collective-permute-done.9.y = bf16[128,1024]{1,0:T(8,128)(2,1)S(1)} collective-permute-done((bf16[128,1024]{1,0:T(8,128)(2,1)}, bf16[128,1024]{1,0:T(8,128)(2,1)S(1)}, u32[]{:S(2)}, u32[]{:S(2)}) %collective-permute-start.9) | collective-permute-done | bytes 262176 | tf_op jit(solution)/shard_map/ppermute | solution.py:322
  17.8 1.7 %collective-permute-start.12 = (bf16[128,1024]{1,0:T(8,128)(2,1)S(1)}, bf16[128,1024]{1,0:T(8,128)(2,1)S(1)}, u32[]{:S(2)}, u32[]{:S(2)}) collective-permute-start(bf16[128,1024]{1,0:T(8,128)(2,1)S(1)} %get-tuple-element.45), channel_id=1, source_target_pairs={{0,1},{1,0},{2,3},{3,2},{4,5},{5,4},{6,7},{7,6},{8,10},{9,11},{10,... | collective-permute-start | bytes 786440 | tf_op jit(solution)/shard_map/ppermute | solution.py:394
  19.6 0.4 collective-permute-start.13
  20.0 0.7 fusion.26.refs_5_.refs_1_
  20.7 0.8 fusion.28.refs_7_.refs_3_
  21.5 2.7 %collective-permute-done.12.a = bf16[128,1024]{1,0:T(8,128)(2,1)S(1)} collective-permute-done((bf16[128,1024]{1,0:T(8,128)(2,1)S(1)}, bf16[128,1024]{1,0:T(8,128)(2,1)S(1)}, u32[]{:S(2)}, u32[]{:S(2)}) %collective-permute-start.12) | collective-permute-done | bytes 262176 | tf_op jit(solution)/shard_map/ppermute | solution.py:394
  24.1 2.8 %collective-permute-done.13.b = bf16[128,1024]{1,0:T(8,128)(2,1)S(1)} collective-permute-done((bf16[128,1024]{1,0:T(8,128)(2,1)S(1)}, bf16[128,1024]{1,0:T(8,128)(2,1)S(1)}, u32[]{:S(2)}, u32[]{:S(2)}) %collective-permute-start.13) | collective-permute-done | bytes 262176 | tf_op jit(solution)/shard_map/ppermute | solution.py:394
  26.9 0.2 shard_map.57
  27.3 0.7 fusion.36.refs_0_.refs_5_
  28.0 0.7 fusion.27.refs_6_.refs_2_
  28.8 0.7 fusion.29.refs_8_.refs_4_
  29.6 0.7 fusion.37.refs_1_.refs_6_
  30.3 1.7 %shard_map.50 = bf16[1024,1024]{1,0:T(8,128)(2,1)S(1)} custom-call(bf16[1024,1024]{1,0:T(8,128)(2,1)} %collective-permute-done.1.value), custom_call_target="tpu_custom_call" | custom-call | flops 1000000 | tf_op jit(solution)/shard_map/pallas_call | solution.py:356
  32.2 1.3 %fusion.1.two.refs_0_ = bf16[1024,512]{1,0:T(8,128)(2,1)S(1)} fusion(bf16[1024,1024]{1,0:T(8,128)(2,1)S(1)} %shard_map.50, bf16[512,1024]{1,0:T(8,128)(2,1)S(1)} %copy-done.1), kind=kOutput, calls=%fused_computation.3 | convolution fusion | flops 1076363264 | bytes 4194304 | tf_op jit(solution)/shard_map/dot_general | solution.py:38
  33.5 0.7 fusion.30.refs_1_
  34.3 0.8 fusion.32.refs_3_
  35.0 0.8 fusion.34.refs_5_
  35.8 0.4 shard_map.51.own
  36.2 1.8 %collective-permute-start.2 = (f32[128,512]{1,0:T(8,128)S(1)}, f32[128,512]{1,0:T(8,128)S(1)}, u32[]{:S(2)}, u32[]{:S(2)}) collective-permute-start(f32[128,512]{1,0:T(8,128)S(1)} %shard_map.51.own), channel_id=1, source_target_pairs={{0,16},{8,24},{16,0},{24,8},{1,17},{9,25},{17,1},{25,9},{2,18},{10... | collective-permute-start | bytes 786440 | tf_op jit(solution)/shard_map/ppermute | solution.py:329
  38.0 0.7 fusion.31.refs_2_
  38.8 0.8 fusion.33.refs_4_
  39.5 5.5 %collective-permute-done.2.got = f32[128,512]{1,0:T(8,128)S(1)} collective-permute-done((f32[128,512]{1,0:T(8,128)S(1)}, f32[128,512]{1,0:T(8,128)S(1)}, u32[]{:S(2)}, u32[]{:S(2)}) %collective-permute-start.2) | collective-permute-done | bytes 262176 | tf_op jit(solution)/shard_map/ppermute | solution.py:329
  45.0 1.8 %collective-permute-start.3 = (f32[32,512]{1,0:T(8,128)S(1)}, f32[32,512]{1,0:T(8,128)S(1)}, u32[]{:S(2)}, u32[]{:S(2)}) collective-permute-start(f32[32,512]{1,0:T(8,128)S(1)} %get-tuple-element.37), channel_id=1, source_target_pairs={{0,1},{1,0},{2,3},{3,2},{4,5},{5,4},{6,7},{7,6},{8,9},{9,8},{10,11... | collective-permute-start | bytes 196616 | tf_op jit(solution)/shard_map/ppermute | solution.py:322
  46.9 1.6 %collective-permute-start.4 = (f32[32,512]{1,0:T(8,128)S(1)}, f32[32,512]{1,0:T(8,128)S(1)}, u32[]{:S(2)}, u32[]{:S(2)}) collective-permute-start(f32[32,512]{1,0:T(8,128)S(1)} %get-tuple-element.38), channel_id=1, source_target_pairs={{0,2},{1,3},{2,0},{3,1},{4,6},{5,7},{6,4},{7,5},{8,10},{9,11},{10,... | collective-permute-start | bytes 196616 | tf_op jit(solution)/shard_map/ppermute | solution.py:322
  48.6 0.7 fusion.35.refs_6_
  49.4 2.1 %collective-permute-done.4.refs_2_ = f32[32,512]{1,0:T(8,128)S(1)} collective-permute-done((f32[32,512]{1,0:T(8,128)S(1)}, f32[32,512]{1,0:T(8,128)S(1)}, u32[]{:S(2)}, u32[]{:S(2)}) %collective-permute-start.4) | collective-permute-done | bytes 65568 | tf_op jit(solution)/shard_map/ppermute | solution.py:322
  51.5 2.1 %collective-permute-done.5.refs_3_ = f32[32,512]{1,0:T(8,128)S(1)} collective-permute-done((f32[32,512]{1,0:T(8,128)S(1)}, f32[32,512]{1,0:T(8,128)S(1)}, u32[]{:S(2)}, u32[]{:S(2)}) %collective-permute-start.5) | collective-permute-done | bytes 65568 | tf_op jit(solution)/shard_map/ppermute | solution.py:322
  53.6 1.0 %shard_map.56 = (f32[32,2048]{1,0:T(8,128)S(1)}, bf16[32,512]{1,0:T(8,128)(2,1)S(1)}, f32[32,1024]{1,0:T(8,128)S(1)}) custom-call(f32[32,512]{1,0:T(8,128)S(1)} %get-tuple-element.36.refs_0_, f32[32,512]{1,0:T(8,128)S(1)} %collective-permute-done.3.refs_1_, f32[32,512]{1,0:T(8,128)S(1)} %collective-permute-done.4.refs_2_, ...), custom_call_target="tpu_custom_call" | custom-call | flops 805306368 | tf_op jit(solution)/shard_map/pallas_call | solution.py:416
  54.6 0.5 shard_map.59
  55.1 2.6 %collective-permute-start.16 = (bf16[32,1024]{1,0:T(8,128)(2,1)S(1)}, bf16[32,1024]{1,0:T(8,128)(2,1)S(1)}, u32[]{:S(2)}, u32[]{:S(2)}) collective-permute-start(bf16[32,1024]{1,0:T(8,128)(2,1)S(1)} %get-tuple-element.52), channel_id=1, source_target_pairs={{0,4},{1,5},{2,6},{3,7},{4,0},{5,1},{6,2},{7,3},{8,12},{9,13},{10,... | collective-permute-start | bytes 196616 | tf_op jit(solution)/shard_map/ppermute | solution.py:329
  57.7 1.3 %shard_map.58 = (f32[32,1024]{1,0:T(8,128)S(1)}, bf16[32,1024]{1,0:T(8,128)(2,1)S(1)}) custom-call(f32[32,2048]{1,0:T(8,128)S(1)} %get-tuple-element.44.direction.right_side, bf16[1024,512]{1,0:T(8,128)(2,1)S(1)} %fusion.1.two.refs_0_, bf16[1024,256]{1,0:T(8,128)(2,1)S(1)} %fusion.30.refs_1_, bf16[1024,256]{1,0:T(8,128)(2,1)S(1)} %fusion.31.refs_2_, ...), custom_call_target="tpu_custom_call" | custom-call | flops 1073741824 | tf_op jit(solution)/shard_map/pallas_call | solution.py:425
  59.0 0.4 collective-permute-start.15
  59.4 2.8 %collective-permute-done.16.got = bf16[32,1024]{1,0:T(8,128)(2,1)S(1)} collective-permute-done((bf16[32,1024]{1,0:T(8,128)(2,1)S(1)}, bf16[32,1024]{1,0:T(8,128)(2,1)S(1)}, u32[]{:S(2)}, u32[]{:S(2)}) %collective-permute-start.16) | collective-permute-done | bytes 65568 | tf_op jit(solution)/shard_map/ppermute | solution.py:329
  62.3 1.3 %shard_map.60 = (f32[32,2048]{1,0:T(8,128)S(1)}, f32[32,128]{1,0:T(8,128)}) custom-call(f32[32,1024]{1,0:T(8,128)S(1)} %get-tuple-element.51.partial, bf16[32,1024]{1,0:T(8,128)(2,1)S(1)} %collective-permute-done.16.got, bf16[1024,512]{1,0:T(8,128)(2,1)S(1)} %fusion.one.refs_4_.refs_0_, bf16[1024,256]{1,0:T(8,128)(2,1)S(1)} %fusion.26.refs_5_.refs_1_, ...), custom_call_target="tpu_custom_call" | custom-call | flops 1073741824 | tf_op jit(solution)/shard_map/pallas_call | solution.py:428
  63.6 1.3 %collective-permute-done.15.got = bf16[32,1024]{1,0:T(8,128)(2,1)S(1)} collective-permute-done((bf16[32,1024]{1,0:T(8,128)(2,1)S(1)}, bf16[32,1024]{1,0:T(8,128)(2,1)S(1)}, u32[]{:S(2)}, u32[]{:S(2)}) %collective-permute-start.15) | collective-permute-done | bytes 65568 | tf_op jit(solution)/shard_map/ppermute | solution.py:329
  64.9 0.8 shard_map.61.own
  65.7 1.5 %collective-permute-start.17 = (f32[32,2048]{1,0:T(8,128)S(1)}, f32[32,2048]{1,0:T(8,128)S(1)}, u32[]{:S(2)}, u32[]{:S(2)}) collective-permute-start(f32[32,2048]{1,0:T(8,128)S(1)} %shard_map.61.own), channel_id=1, source_target_pairs={{0,16},{8,24},{16,0},{24,8},{1,17},{9,25},{17,1},{25,9},{2,18},{10... | collective-permute-start | bytes 786440 | tf_op jit(solution)/shard_map/ppermute | solution.py:329
  67.2 4.9 %collective-permute-done.17.got = f32[32,2048]{1,0:T(8,128)S(1)} collective-permute-done((f32[32,2048]{1,0:T(8,128)S(1)}, f32[32,2048]{1,0:T(8,128)S(1)}, u32[]{:S(2)}, u32[]{:S(2)}) %collective-permute-start.17) | collective-permute-done | bytes 262176 | tf_op jit(solution)/shard_map/ppermute | solution.py:329
  72.3 4.6 %collective-permute-done.18.got_sums = f32[32,128]{1,0:T(8,128)S(1)} collective-permute-done((f32[32,128]{1,0:T(8,128)S(1)}, f32[32,128]{1,0:T(8,128)S(1)}, u32[]{:S(2)}, u32[]{:S(2)}) %collective-permute-start.18) | collective-permute-done | bytes 16416 | tf_op jit(solution)/shard_map/ppermute | solution.py:329
  76.9 1.4 %shard_map.63 = (f32[32,2048]{1,0:T(8,128)S(1)}, f32[32,2048]{1,0:T(8,128)S(1)}, f32[32,1024]{1,0:T(8,128)S(1)}, bf16[32,1024]{1,0:T(8,128)(2,1)S(1)}) custom-call(f32[32,128]{1,0:T(8,128)S(1)} %get-tuple-element.54.own_sums, f32[32,128]{1,0:T(8,128)S(1)} %collective-permute-done.18.got_sums, f32[32,2048]{1,0:T(8,128)S(1)} %get-tuple-element.44.direction.right_side, ...), custom_call_target="tpu_custom_call" | custom-call | flops 1073741824 | tf_op jit(solution)/shard_map/pallas_call | solution.py:435
  78.4 1.3 %shard_map.64 = (f32[32,1024]{1,0:T(8,128)S(1)}, bf16[32,1024]{1,0:T(8,128)(2,1)S(1)}) custom-call(f32[32,2048]{1,0:T(8,128)S(1)} %get-tuple-element.56.direction, bf16[1024,512]{1,0:T(8,128)(2,1)S(1)} %fusion.1.two.refs_0_, bf16[1024,256]{1,0:T(8,128)(2,1)S(1)} %fusion.30.refs_1_, bf16[1024,256]{1,0:T(8,128)(2,1)S(1)} %fusion.31.refs_2_, ...), custom_call_target="tpu_custom_call" | custom-call | flops 1073741824 | tf_op jit(solution)/shard_map/pallas_call | solution.py:439
  79.7 3.0 %collective-permute-start.19 = (bf16[32,1024]{1,0:T(8,128)(2,1)S(1)}, bf16[32,1024]{1,0:T(8,128)(2,1)S(1)}, u32[]{:S(2)}, u32[]{:S(2)}) collective-permute-start(bf16[32,1024]{1,0:T(8,128)(2,1)S(1)} %get-tuple-element.58), channel_id=1, source_target_pairs={{0,4},{1,5},{2,6},{3,7},{4,0},{5,1},{6,2},{7,3},{8,12},{9,13},{10,... | collective-permute-start | bytes 196616 | tf_op jit(solution)/shard_map/ppermute | solution.py:329
  82.7 1.1 %collective-permute-done.20.got = bf16[32,1024]{1,0:T(8,128)(2,1)S(1)} collective-permute-done((bf16[32,1024]{1,0:T(8,128)(2,1)S(1)}, bf16[32,1024]{1,0:T(8,128)(2,1)S(1)}, u32[]{:S(2)}, u32[]{:S(2)}) %collective-permute-start.20) | collective-permute-done | bytes 65568 | tf_op jit(solution)/shard_map/ppermute | solution.py:329
  83.8 0.8 shard_map.65
  84.6 0.8 collective-permute-done.19.got
  85.4 0.8 shard_map.66
  86.3 1.6 %collective-permute-start.21 = (bf16[32,2176]{1,0:T(8,128)(2,1)S(1)}, bf16[32,2176]{1,0:T(8,128)(2,1)S(1)}, u32[]{:S(2)}, u32[]{:S(2)}) collective-permute-start(bf16[32,2176]{1,0:T(8,128)(2,1)S(1)} %get-tuple-element.63.low), channel_id=1, source_target_pairs={{0,16},{8,24},{16,0},{24,8},{1,17},{9,25},{17,1},{25,9},{2,18},{10... | collective-permute-start | bytes 417800 | tf_op jit(solution)/shard_map/ppermute | solution.py:329
  87.8 3.6 %collective-permute-done.21.got = bf16[32,2176]{1,0:T(8,128)(2,1)S(1)} collective-permute-done((bf16[32,2176]{1,0:T(8,128)(2,1)S(1)}, bf16[32,2176]{1,0:T(8,128)(2,1)S(1)}, u32[]{:S(2)}, u32[]{:S(2)}) %collective-permute-start.21) | collective-permute-done | bytes 139296 | tf_op jit(solution)/shard_map/ppermute | solution.py:329
  91.4 0.2 shard_map.67
  91.6 1.1 %collective-permute-start.22 = (bf16[64,512]{1,0:T(8,128)(2,1)S(1)}, bf16[64,512]{1,0:T(8,128)(2,1)S(1)}, u32[]{:S(2)}, u32[]{:S(2)}) collective-permute-start(bf16[64,512]{1,0:T(8,128)(2,1)S(1)} %get-tuple-element.67), channel_id=1, source_target_pairs={{0,1},{1,0},{2,3},{3,2},{4,5},{5,4},{6,7},{7,6},{8,9},{9,8},{10,11... | collective-permute-start | bytes 196616 | tf_op jit(solution)/shard_map/ppermute | solution.py:322
  92.8 2.4 %collective-permute-start.24 = (bf16[64,512]{1,0:T(8,128)(2,1)S(1)}, bf16[64,512]{1,0:T(8,128)(2,1)S(1)}, u32[]{:S(2)}, u32[]{:S(2)}) collective-permute-start(bf16[64,512]{1,0:T(8,128)(2,1)S(1)} %get-tuple-element.69), channel_id=1, source_target_pairs={{0,3},{1,2},{2,1},{3,0},{4,7},{5,6},{6,5},{7,4},{8,11},{9,10},{10,... | collective-permute-start | bytes 196616 | tf_op jit(solution)/shard_map/ppermute | solution.py:322
  95.2 0.8 collective-permute-done.22.refs_1_
  96.0 1.0 collective-permute-done.23.refs_2_
  97.0 1.2 %collective-permute-done.24.refs_3_ = bf16[64,512]{1,0:T(8,128)(2,1)S(1)} collective-permute-done((bf16[64,512]{1,0:T(8,128)(2,1)S(1)}, bf16[64,512]{1,0:T(8,128)(2,1)S(1)}, u32[]{:S(2)}, u32[]{:S(2)}) %collective-permute-start.24) | collective-permute-done | bytes 65568 | tf_op jit(solution)/shard_map/ppermute | solution.py:322
  98.2 1.2 %collective-permute-done.28.refs_7_ = bf16[64,512]{1,0:T(8,128)(2,1)S(1)} collective-permute-done((bf16[64,512]{1,0:T(8,128)(2,1)S(1)}, bf16[64,512]{1,0:T(8,128)(2,1)S(1)}, u32[]{:S(2)}, u32[]{:S(2)}) %collective-permute-start.28) | collective-permute-done | bytes 65568 | tf_op jit(solution)/shard_map/ppermute | solution.py:319
  99.4 1.1 %shard_map.68 = (f32[512,256]{1,0:T(8,128)}, f32[512,256]{1,0:T(8,128)}) custom-call(bf16[64,512]{1,0:T(8,128)(2,1)S(1)} %get-tuple-element.66.refs_0_, bf16[64,512]{1,0:T(8,128)(2,1)S(1)} %collective-permute-done.22.refs_1_, bf16[64,512]{1,0:T(8,128)(2,1)S(1)} %collective-permute-done.23.refs_2_, bf16[64,512]{1,0:T(8,128)(2,1)S(1)} %collective-permute-done.24.refs_3_, ...), custom_call_target="tpu_custom_call" | custom-call | flops 1000000 | tf_op jit(solution)/shard_map/pallas_call | solution.py:454
  (40 shorter events, 1.3 us)
Async XLA Ops:
  0.6 10.4 %copy-start = (bf16[1024,256]{1,0:T(8,128)(2,1)S(1)}, bf16[1024,256]{1,0:T(8,128)(2,1)}, u32[]{:S(2)}) copy-start(bf16[1024,256]{1,0:T(8,128)(2,1)} %param.5) | copy-start | bytes 1572868
  2.6 10.4 %collective-permute-start.6 = (bf16[128,1024]{1,0:T(8,128)(2,1)}, bf16[128,1024]{1,0:T(8,128)(2,1)S(1)}, u32[]{:S(2)}, u32[]{:S(2)}) collective-permute-start(bf16[128,1024]{1,0:T(8,128)(2,1)} %get-tuple-element.40), channel_id=1, source_target_pairs={{0,1},{1,0},{2,3},{3,2},{4,5},{5,4},{6,7},{7,6},{8,9},{9,8},{10,11... | collective-permute-start | bytes 786440 | tf_op jit(solution)/shard_map/ppermute | solution.py:322
  5.6 9.4 %collective-permute-start.7 = (bf16[128,1024]{1,0:T(8,128)(2,1)}, bf16[128,1024]{1,0:T(8,128)(2,1)S(1)}, u32[]{:S(2)}, u32[]{:S(2)}) collective-permute-start(bf16[128,1024]{1,0:T(8,128)(2,1)} %get-tuple-element.40), channel_id=1, source_target_pairs={{0,2},{1,3},{2,0},{3,1},{4,6},{5,7},{6,4},{7,5},{8,10},{9,11},{10,... | collective-permute-start | bytes 786440 | tf_op jit(solution)/shard_map/ppermute | solution.py:322
  7.2 10.6 %collective-permute-start.9 = (bf16[128,1024]{1,0:T(8,128)(2,1)}, bf16[128,1024]{1,0:T(8,128)(2,1)S(1)}, u32[]{:S(2)}, u32[]{:S(2)}) collective-permute-start(bf16[128,1024]{1,0:T(8,128)(2,1)} %get-tuple-element.42), channel_id=1, source_target_pairs={{0,1},{1,0},{2,3},{3,2},{4,5},{5,4},{6,7},{7,6},{8,9},{9,8},{10,11... | collective-permute-start | bytes 786440 | tf_op jit(solution)/shard_map/ppermute | solution.py:322
  7.7 11.8 %collective-permute-start.10 = (bf16[128,1024]{1,0:T(8,128)(2,1)}, bf16[128,1024]{1,0:T(8,128)(2,1)S(1)}, u32[]{:S(2)}, u32[]{:S(2)}) collective-permute-start(bf16[128,1024]{1,0:T(8,128)(2,1)} %get-tuple-element.42), channel_id=1, source_target_pairs={{0,2},{1,3},{2,0},{3,1},{4,6},{5,7},{6,4},{7,5},{8,10},{9,11},{10,... | collective-permute-start | bytes 786440 | tf_op jit(solution)/shard_map/ppermute | solution.py:322
  7.7 22.6 %collective-permute-start.1 = (bf16[1024,1024]{1,0:T(8,128)(2,1)}, bf16[1024,1024]{1,0:T(8,128)(2,1)}, u32[]{:S(2)}, u32[]{:S(2)}) collective-permute-start(bf16[1024,1024]{1,0:T(8,128)(2,1)} %param.3), channel_id=1, source_target_pairs={{0,8},{8,0},{16,24},{24,16},{1,9},{9,1},{17,25},{25,17},{2,10},{10... | collective-permute-start | bytes 6291464 | tf_op jit(solution)/shard_map/ppermute | solution.py:319
  11.0 8.9 %copy-start.2 = (bf16[1024,1024]{1,0:T(8,128)(2,1)S(1)}, bf16[1024,1024]{1,0:T(8,128)(2,1)}, u32[]{:S(2)}) copy-start(bf16[1024,1024]{1,0:T(8,128)(2,1)} %param.3) | copy-start | bytes 6291460
  13.0 22.8 %collective-permute-start = (bf16[128,1024]{1,0:T(8,128)(2,1)S(1)}, bf16[128,1024]{1,0:T(8,128)(2,1)S(1)}, u32[]{:S(2)}, u32[]{:S(2)}) collective-permute-start(bf16[128,1024]{1,0:T(8,128)(2,1)S(1)} %get-tuple-element.70), channel_id=1, source_target_pairs={{0,8},{8,0},{16,24},{24,16},{1,9},{9,1},{17,25},{25,17},{2,10},{10... | collective-permute-start | bytes 786440 | tf_op jit(solution)/shard_map/ppermute | solution.py:319
  15.1 12.9 %collective-permute-start.8 = (bf16[256,1024]{1,0:T(8,128)(2,1)S(1)}, bf16[256,1024]{1,0:T(8,128)(2,1)S(1)}, u32[]{:S(2)}, u32[]{:S(2)}) collective-permute-start(bf16[256,1024]{1,0:T(8,128)(2,1)S(1)} %get-tuple-element.41), channel_id=1, source_target_pairs={{0,8},{8,0},{16,24},{24,16},{1,9},{9,1},{17,25},{25,17},{2,10},{10... | collective-permute-start | bytes 1572872 | tf_op jit(solution)/shard_map/ppermute | solution.py:319
  17.8 6.4 %collective-permute-start.12 = (bf16[128,1024]{1,0:T(8,128)(2,1)S(1)}, bf16[128,1024]{1,0:T(8,128)(2,1)S(1)}, u32[]{:S(2)}, u32[]{:S(2)}) collective-permute-start(bf16[128,1024]{1,0:T(8,128)(2,1)S(1)} %get-tuple-element.45), channel_id=1, source_target_pairs={{0,1},{1,0},{2,3},{3,2},{4,5},{5,4},{6,7},{7,6},{8,10},{9,11},{10,... | collective-permute-start | bytes 786440 | tf_op jit(solution)/shard_map/ppermute | solution.py:394
  19.6 7.3 %collective-permute-start.13 = (bf16[128,1024]{1,0:T(8,128)(2,1)S(1)}, bf16[128,1024]{1,0:T(8,128)(2,1)S(1)}, u32[]{:S(2)}, u32[]{:S(2)}) collective-permute-start(bf16[128,1024]{1,0:T(8,128)(2,1)S(1)} %get-tuple-element.46), channel_id=1, source_target_pairs={{0,1},{1,0},{2,3},{3,2},{4,5},{5,4},{6,7},{7,6},{8,10},{9,11},{10,... | collective-permute-start | bytes 786440 | tf_op jit(solution)/shard_map/ppermute | solution.py:394
  24.1 4.7 %collective-permute-start.11 = (bf16[256,1024]{1,0:T(8,128)(2,1)S(1)}, bf16[256,1024]{1,0:T(8,128)(2,1)S(1)}, u32[]{:S(2)}, u32[]{:S(2)}) collective-permute-start(bf16[256,1024]{1,0:T(8,128)(2,1)S(1)} %get-tuple-element.43), channel_id=1, source_target_pairs={{0,8},{8,0},{16,24},{24,16},{1,9},{9,1},{17,25},{25,17},{2,10},{10... | collective-permute-start | bytes 1572872 | tf_op jit(solution)/shard_map/ppermute | solution.py:319
  27.2 2.4 %collective-permute-start.14 = (bf16[256,1024]{1,0:T(8,128)(2,1)S(1)}, bf16[256,1024]{1,0:T(8,128)(2,1)S(1)}, u32[]{:S(2)}, u32[]{:S(2)}) collective-permute-start(bf16[256,1024]{1,0:T(8,128)(2,1)S(1)} %shard_map.57), channel_id=1, source_target_pairs={{0,8},{8,0},{16,24},{24,16},{1,9},{9,1},{17,25},{25,17},{2,10},{10... | collective-permute-start | bytes 1572872 | tf_op jit(solution)/shard_map/ppermute | solution.py:319
  30.3 1.9 %copy-start.1 = (bf16[512,1024]{1,0:T(8,128)(2,1)S(1)}, bf16[512,1024]{1,0:T(8,128)(2,1)}, u32[]{:S(2)}) copy-start(bf16[512,1024]{1,0:T(8,128)(2,1)} %centers.1) | copy-start | bytes 3145732
  36.2 8.8 %collective-permute-start.2 = (f32[128,512]{1,0:T(8,128)S(1)}, f32[128,512]{1,0:T(8,128)S(1)}, u32[]{:S(2)}, u32[]{:S(2)}) collective-permute-start(f32[128,512]{1,0:T(8,128)S(1)} %shard_map.51.own), channel_id=1, source_target_pairs={{0,16},{8,24},{16,0},{24,8},{1,17},{9,25},{17,1},{25,9},{2,18},{10... | collective-permute-start | bytes 786440 | tf_op jit(solution)/shard_map/ppermute | solution.py:329
  45.0 4.3 %collective-permute-start.3 = (f32[32,512]{1,0:T(8,128)S(1)}, f32[32,512]{1,0:T(8,128)S(1)}, u32[]{:S(2)}, u32[]{:S(2)}) collective-permute-start(f32[32,512]{1,0:T(8,128)S(1)} %get-tuple-element.37), channel_id=1, source_target_pairs={{0,1},{1,0},{2,3},{3,2},{4,5},{5,4},{6,7},{7,6},{8,9},{9,8},{10,11... | collective-permute-start | bytes 196616 | tf_op jit(solution)/shard_map/ppermute | solution.py:322
  46.9 4.6 %collective-permute-start.4 = (f32[32,512]{1,0:T(8,128)S(1)}, f32[32,512]{1,0:T(8,128)S(1)}, u32[]{:S(2)}, u32[]{:S(2)}) collective-permute-start(f32[32,512]{1,0:T(8,128)S(1)} %get-tuple-element.38), channel_id=1, source_target_pairs={{0,2},{1,3},{2,0},{3,1},{4,6},{5,7},{6,4},{7,5},{8,10},{9,11},{10,... | collective-permute-start | bytes 196616 | tf_op jit(solution)/shard_map/ppermute | solution.py:322
  48.4 5.2 %collective-permute-start.5 = (f32[32,512]{1,0:T(8,128)S(1)}, f32[32,512]{1,0:T(8,128)S(1)}, u32[]{:S(2)}, u32[]{:S(2)}) collective-permute-start(f32[32,512]{1,0:T(8,128)S(1)} %get-tuple-element.39), channel_id=1, source_target_pairs={{0,3},{1,2},{2,1},{3,0},{4,7},{5,6},{6,5},{7,4},{8,11},{9,10},{10,... | collective-permute-start | bytes 196616 | tf_op jit(solution)/shard_map/ppermute | solution.py:322
  55.1 7.2 %collective-permute-start.16 = (bf16[32,1024]{1,0:T(8,128)(2,1)S(1)}, bf16[32,1024]{1,0:T(8,128)(2,1)S(1)}, u32[]{:S(2)}, u32[]{:S(2)}) collective-permute-start(bf16[32,1024]{1,0:T(8,128)(2,1)S(1)} %get-tuple-element.52), channel_id=1, source_target_pairs={{0,4},{1,5},{2,6},{3,7},{4,0},{5,1},{6,2},{7,3},{8,12},{9,13},{10,... | collective-permute-start | bytes 196616 | tf_op jit(solution)/shard_map/ppermute | solution.py:329
  59.0 5.8 %collective-permute-start.15 = (bf16[32,1024]{1,0:T(8,128)(2,1)S(1)}, bf16[32,1024]{1,0:T(8,128)(2,1)S(1)}, u32[]{:S(2)}, u32[]{:S(2)}) collective-permute-start(bf16[32,1024]{1,0:T(8,128)(2,1)S(1)} %get-tuple-element.48), channel_id=1, source_target_pairs={{0,4},{1,5},{2,6},{3,7},{4,0},{5,1},{6,2},{7,3},{8,12},{9,13},{10,... | collective-permute-start | bytes 196616 | tf_op jit(solution)/shard_map/ppermute | solution.py:329
  65.7 6.4 %collective-permute-start.17 = (f32[32,2048]{1,0:T(8,128)S(1)}, f32[32,2048]{1,0:T(8,128)S(1)}, u32[]{:S(2)}, u32[]{:S(2)}) collective-permute-start(f32[32,2048]{1,0:T(8,128)S(1)} %shard_map.61.own), channel_id=1, source_target_pairs={{0,16},{8,24},{16,0},{24,8},{1,17},{9,25},{17,1},{25,9},{2,18},{10... | collective-permute-start | bytes 786440 | tf_op jit(solution)/shard_map/ppermute | solution.py:329
  72.2 4.7 %collective-permute-start.18 = (f32[32,128]{1,0:T(8,128)S(1)}, f32[32,128]{1,0:T(8,128)S(1)}, u32[]{:S(2)}, u32[]{:S(2)}) collective-permute-start(f32[32,128]{1,0:T(8,128)S(1)} %get-tuple-element.54.own_sums), channel_id=1, source_target_pairs={{0,4},{1,5},{2,6},{3,7},{4,0},{5,1},{6,2},{7,3},{8,12},{9,13},{10,... | collective-permute-start | bytes 49160 | tf_op jit(solution)/shard_map/ppermute | solution.py:329
  78.4 5.5 %collective-permute-start.20 = (bf16[32,1024]{1,0:T(8,128)(2,1)S(1)}, bf16[32,1024]{1,0:T(8,128)(2,1)S(1)}, u32[]{:S(2)}, u32[]{:S(2)}) collective-permute-start(bf16[32,1024]{1,0:T(8,128)(2,1)S(1)} %get-tuple-element.60), channel_id=1, source_target_pairs={{0,4},{1,5},{2,6},{3,7},{4,0},{5,1},{6,2},{7,3},{8,12},{9,13},{10,... | collective-permute-start | bytes 196616 | tf_op jit(solution)/shard_map/ppermute | solution.py:329
  79.7 5.7 %collective-permute-start.19 = (bf16[32,1024]{1,0:T(8,128)(2,1)S(1)}, bf16[32,1024]{1,0:T(8,128)(2,1)S(1)}, u32[]{:S(2)}, u32[]{:S(2)}) collective-permute-start(bf16[32,1024]{1,0:T(8,128)(2,1)S(1)} %get-tuple-element.58), channel_id=1, source_target_pairs={{0,4},{1,5},{2,6},{3,7},{4,0},{5,1},{6,2},{7,3},{8,12},{9,13},{10,... | collective-permute-start | bytes 196616 | tf_op jit(solution)/shard_map/ppermute | solution.py:329
  86.3 5.1 %collective-permute-start.21 = (bf16[32,2176]{1,0:T(8,128)(2,1)S(1)}, bf16[32,2176]{1,0:T(8,128)(2,1)S(1)}, u32[]{:S(2)}, u32[]{:S(2)}) collective-permute-start(bf16[32,2176]{1,0:T(8,128)(2,1)S(1)} %get-tuple-element.63.low), channel_id=1, source_target_pairs={{0,16},{8,24},{16,0},{24,8},{1,17},{9,25},{17,1},{25,9},{2,18},{10... | collective-permute-start | bytes 417800 | tf_op jit(solution)/shard_map/ppermute | solution.py:329
  91.6 4.3 %collective-permute-start.22 = (bf16[64,512]{1,0:T(8,128)(2,1)S(1)}, bf16[64,512]{1,0:T(8,128)(2,1)S(1)}, u32[]{:S(2)}, u32[]{:S(2)}) collective-permute-start(bf16[64,512]{1,0:T(8,128)(2,1)S(1)} %get-tuple-element.67), channel_id=1, source_target_pairs={{0,1},{1,0},{2,3},{3,2},{4,5},{5,4},{6,7},{7,6},{8,9},{9,8},{10,11... | collective-permute-start | bytes 196616 | tf_op jit(solution)/shard_map/ppermute | solution.py:322
  92.7 4.3 %collective-permute-start.23 = (bf16[64,512]{1,0:T(8,128)(2,1)S(1)}, bf16[64,512]{1,0:T(8,128)(2,1)S(1)}, u32[]{:S(2)}, u32[]{:S(2)}) collective-permute-start(bf16[64,512]{1,0:T(8,128)(2,1)S(1)} %get-tuple-element.68), channel_id=1, source_target_pairs={{0,2},{1,3},{2,0},{3,1},{4,6},{5,7},{6,4},{7,5},{8,10},{9,11},{10,... | collective-permute-start | bytes 196616 | tf_op jit(solution)/shard_map/ppermute | solution.py:322
  92.8 5.3 %collective-permute-start.24 = (bf16[64,512]{1,0:T(8,128)(2,1)S(1)}, bf16[64,512]{1,0:T(8,128)(2,1)S(1)}, u32[]{:S(2)}, u32[]{:S(2)}) collective-permute-start(bf16[64,512]{1,0:T(8,128)(2,1)S(1)} %get-tuple-element.69), channel_id=1, source_target_pairs={{0,3},{1,2},{2,1},{3,0},{4,7},{5,6},{6,5},{7,4},{8,11},{9,10},{10,... | collective-permute-start | bytes 196616 | tf_op jit(solution)/shard_map/ppermute | solution.py:322
  95.2 2.9 %collective-permute-start.25 = (bf16[64,512]{1,0:T(8,128)(2,1)S(1)}, bf16[64,512]{1,0:T(8,128)(2,1)S(1)}, u32[]{:S(2)}, u32[]{:S(2)}) collective-permute-start(bf16[64,512]{1,0:T(8,128)(2,1)S(1)} %get-tuple-element.66.refs_0_), channel_id=1, source_target_pairs={{0,8},{8,0},{16,24},{24,16},{1,9},{9,1},{17,25},{25,17},{2,10},{10... | collective-permute-start | bytes 196616 | tf_op jit(solution)/shard_map/ppermute | solution.py:319
  96.0 2.2 %collective-permute-start.26 = (bf16[64,512]{1,0:T(8,128)(2,1)S(1)}, bf16[64,512]{1,0:T(8,128)(2,1)S(1)}, u32[]{:S(2)}, u32[]{:S(2)}) collective-permute-start(bf16[64,512]{1,0:T(8,128)(2,1)S(1)} %collective-permute-done.22.refs_1_), channel_id=1, source_target_pairs={{0,8},{8,0},{16,24},{24,16},{1,9},{9,1},{17,25},{25,17},{2,10},{10... | collective-permute-start | bytes 196616 | tf_op jit(solution)/shard_map/ppermute | solution.py:319
  97.0 1.3 %collective-permute-start.27 = (bf16[64,512]{1,0:T(8,128)(2,1)S(1)}, bf16[64,512]{1,0:T(8,128)(2,1)S(1)}, u32[]{:S(2)}, u32[]{:S(2)}) collective-permute-start(bf16[64,512]{1,0:T(8,128)(2,1)S(1)} %collective-permute-done.23.refs_2_), channel_id=1, source_target_pairs={{0,8},{8,0},{16,24},{24,16},{1,9},{9,1},{17,25},{25,17},{2,10},{10... | collective-permute-start | bytes 196616 | tf_op jit(solution)/shard_map/ppermute | solution.py:319
  98.1 1.3 %collective-permute-start.28 = (bf16[64,512]{1,0:T(8,128)(2,1)S(1)}, bf16[64,512]{1,0:T(8,128)(2,1)S(1)}, u32[]{:S(2)}, u32[]{:S(2)}) collective-permute-start(bf16[64,512]{1,0:T(8,128)(2,1)S(1)} %collective-permute-done.24.refs_3_), channel_id=1, source_target_pairs={{0,8},{8,0},{16,24},{24,16},{1,9},{9,1},{17,25},{25,17},{2,10},{10... | collective-permute-start | bytes 196616 | tf_op jit(solution)/shard_map/ppermute | solution.py:319
